TPU v7x, 256 devices: a whole 4x4x8 slice. The times are simulated.
256 devices in a mesh: rows: 4 (over x), grid: 64 (over z, y, core).
Axes of the slice: x: 4, y: 4, z: 8, core: 2. Of those that a mesh axis runs over, the one named last changes fastest.
Arguments:
- positions: int32 [2, 2048], P(None, 'rows'), may hold values from 0 to 63, as said below
- angles: int32 [2, 32768], P(None, 'grid'), may hold values from 0 to 4095
- subspace: bfloat16 [2, 2048, 1920], P(None, 'rows', 'grid')
Outputs:
- spectrum: float32 [32768], P('grid')
Inputs may be any that keep to these rules, and one draw needn't show every extreme that they name: `positions`: each column names a distinct lattice point; both coordinates lie in 0 to 63.
All inputs are finite; a program needn't handle non-finite values.
Results may differ from a plain program's by a relative error of at most 0.0012.
Values may be sent and summed in bfloat16 or wider, within the bound.
No kernel may reach another device: no remote copies, remote signals or barrier semaphores. Data moves between devices by JAX's collectives and lax.ppermute only.
A program may use at most 64 MiB of HBM per device.

v0:
```python
import math

import jax
import jax.numpy as jnp
from jax import lax
from jax.sharding import Mesh
from jax.sharding import PartitionSpec as P

NOISE = 1920
PHASES = 4096
GRID = ("grid_0", "grid_1", "grid_2")


def joined_along(pieces, dim):
    shape = list(pieces.shape[1:])
    shape[dim] *= pieces.shape[0]
    return jnp.moveaxis(pieces, 0, dim).reshape(shape)


def all_blocks(array, axes, turns):
    pieces = array[None]
    for k in turns:
        pieces = lax.all_gather(pieces, axes[k], axis=0, tiled=True)
    block = [lax.axis_size(axes[k]) for k in reversed(turns)]
    pieces = pieces.reshape(*block, *array.shape)
    turned = sorted(range(len(turns)), key=lambda place: turns[len(turns) - 1 - place])
    return pieces.transpose(*turned, *range(len(turns), pieces.ndim)).reshape(-1, *array.shape)


def whole_of(array, axes, turns, dim):
    return joined_along(all_blocks(array, axes, turns), dim)


def from_everyone(array, axis):
    devices = lax.axis_size(axis)
    return lax.all_to_all(
        jnp.broadcast_to(array[None], (devices, *array.shape)), axis, 0, 0, tiled=True
    )


def gather_directly(array, axis, dim):
    pieces = from_everyone(array, axis)
    return joined_along(pieces, dim)


def taken_together(array, axis):
    everything = from_everyone(array, axis)
    return jnp.sum(everything, axis=0)


def steering_block(positions, angle_block):
    phase_index = (
        positions[0][:, None] * angle_block[0][None, :]
        + positions[1][:, None] * angle_block[1][None, :]
    ) % PHASES
    phase = phase_index.astype(jnp.float32) * (2.0 * math.pi / PHASES)
    return jnp.concatenate([jnp.cos(phase), jnp.sin(phase)], 0).astype(jnp.bfloat16)


def project_with(column_piece, steering):
    real_part = column_piece[0]
    imag_part = column_piece[1]
    upper_half = jnp.concatenate([real_part, imag_part], 0)
    lower_half = jnp.concatenate([-imag_part, real_part], 0)
    stacked = jnp.stack([upper_half, lower_half])
    return jnp.einsum("pmk,ma->pka", stacked, steering, preferred_element_type=jnp.float32)


def body(positions, angles, subspace):
    whole_columns = whole_of(subspace, GRID, (1, 0, 2), 2)
    column_share = lax.all_to_all(whole_columns, "rows", split_axis=2, concat_axis=1, tiled=True)
    all_positions = gather_directly(positions, "rows", 1)
    steering = steering_block(all_positions, angles)
    projected = project_with(column_share, steering)
    squares = taken_together(jnp.sum(projected * projected, axis=(0, 1)), "rows")
    return 1.0 / (squares / NOISE + 1e-06)


def solution(mesh):
    split = Mesh(
        mesh.devices.reshape(mesh.shape["rows"], 8, 4, 2), ("rows", "grid_0", "grid_1", "grid_2")
    )
    in_specs = (P(None, "rows"), P(None, GRID), P(None, "rows", GRID))
    out_specs = P(GRID)
    return jax.shard_map(body, mesh=split, in_specs=in_specs, out_specs=out_specs, check_vma=False)
```

profile of v0, /device:TPU:8, one launch (start us, length us, event | category | flops | bytes accessed | tf_op | source)
XLA Modules:
  0.0 170.5 jit_solution(8098064754256414551)
XLA Ops:
  6.5 0.0 all-gather.4.cloned.1.call-start
  6.5 0.8 copy.24
  7.4 12.5 %all-gather = bf16[8,512,30]{1,2,0:T(8,128)(2,1)S(1)} all-gather(bf16[2,512,30]{1,2,0:T(8,128)(2,1)S(1)} %copy.24), channel_id=2, replica_groups=mesh['rows'=4,'grid_0'=8,'grid_1'=4,'grid_2'=2] {'grid_1'}, dimensions={0}, use_global_device_ids=true | all-gather | bytes 307200 | tf_op jit(solution)/shard_map/all_gather | solution.py:23
  19.9 1.0 copy.25
  20.9 0.0 all-gather.4.cloned.1.call-update
  20.9 0.0 all-gather.6.cloned.1.call-start
  20.9 43.4 %all-gather.4.cloned.1.call-done = bf16[32,2,512,30]{2,1,3,0:T(2,128)(2,1)} async-done(((bf16[4,2,512,30]{2,1,3,0:T(2,128)(2,1)}), bf16[32,2,512,30]{2,1,3,0:T(2,128)(2,1)}) %all-gather.4.cloned.1.call-update) | async-done | bytes 1966096 | tf_op jit(solution)/shard_map/all_gather | solution.py:23
  64.3 0.0 all-gather.6.cloned.1.call-update
  64.3 1.3 broadcast_in_dim.7
  65.6 4.2 %all-to-all-start.1 = ((s32[4,2,512]{2,1,0:T(2,128)}), s32[4,2,512]{2,1,0:T(2,128)S(1)}, u32[]{:S(2)}, u32[]{:S(2)}) async-start(s32[4,2,512]{2,1,0:T(2,128)} %broadcast_in_dim.7), calls=%async_computation.1 | async-start | bytes 32768 | tf_op jit(solution)/shard_map/all_to_all | solution.py:36
  69.9 13.3 %all-gather.6.cloned.1.call-done = bf16[64,2,512,30]{2,1,3,0:T(2,128)(2,1)} async-done(((bf16[32,2,512,30]{2,1,3,0:T(2,128)(2,1)}), bf16[64,2,512,30]{2,1,3,0:T(2,128)(2,1)}) %all-gather.6.cloned.1.call-update) | async-done | bytes 3932176 | tf_op jit(solution)/shard_map/all_gather | solution.py:23
  83.2 6.9 %copy.26 = bf16[8,4,2,2,512,30]{4,3,5,2,1,0:T(2,128)(2,1)} copy(bf16[8,4,2,2,512,30]{4,3,5,1,0,2:T(2,128)(2,1)} %bitcast.43) | data formatting | bytes 7864320 | tf_op jit(solution)/shard_map/transpose | solution.py:27
  90.1 0.0 all-to-all-done.1
  90.1 0.0 copy-start.1
  90.1 5.1 %all-to-all-start = ((bf16[2,512,1920]{1,0,2:T(2,128)(2,1)}), bf16[2,512,1920]{1,0,2:T(2,128)(2,1)}, u32[]{:S(2)}, u32[]{:S(2)}) async-start(bf16[2,512,1920]{1,0,2:T(2,128)(2,1)} %bitcast.38), calls=%async_computation | async-start | bytes 7864320 | tf_op jit(solution)/shard_map/all_to_all | solution.py:71
  95.3 0.0 copy-done.1
  95.3 19.3 %cosine_convert_fusion = (bf16[2048,512]{1,0:T(8,128)(2,1)S(1)}, bf16[2048,512]{1,0:T(8,128)(2,1)}) fusion(s32[512]{0:T(512)S(1)} %bitcast.49, s32[2048]{0:T(1024)S(1)} %bitcast.47, s32[512]{0:T(512)S(1)} %bitcast.48, s32[2048]{0:T(1024)S(1)} %bitcast.46), kind=kLoop, calls=%fused_computation.14 | loop fusion | flops 18874368 | bytes 4214784 | tf_op jit(solution)/shard_map/convert
  114.6 27.2 %all-to-all-done = bf16[2,512,1920]{1,0,2:T(2,128)(2,1)} async-done(((bf16[2,512,1920]{1,0,2:T(2,128)(2,1)}), bf16[2,512,1920]{1,0,2:T(2,128)(2,1)}, u32[]{:S(2)}, u32[]{:S(2)}) %all-to-all-start) | async-done | bytes 3932192 | tf_op jit(solution)/shard_map/all_to_all | solution.py:71
  141.9 2.7 %copy.27 = bf16[2,512,1920]{1,2,0:T(8,128)(2,1)S(1)} copy(bf16[2,512,1920]{1,0,2:T(2,128)(2,1)} %all-to-all-done) | data formatting | bytes 7864320 | tf_op jit(solution)/shard_map/all_to_all | solution.py:71
  144.6 0.3 fusion.12
  144.9 1.5 copy.29
  146.4 0.6 copy.33
  147.0 0.5 neg.3
  147.5 1.5 copy.28
  149.0 0.6 copy.32
  149.6 0.0 copy-start
  149.6 0.9 maximum_bitcast_fusion.2
  150.5 0.6 copy-done
  151.2 4.2 %multiply_reduce_fusion = f32[512]{0:T(512)S(1)} fusion(bf16[2048,512]{1,0:T(8,128)(2,1)S(1)} %copy-done, bf16[2048,512]{1,0:T(8,128)(2,1)S(1)} %get-tuple-element.9, bf16[1,4096,480]{1,2,0:T(8,128)(2,1)S(1)} %get-tuple-element.8, bf16[1,4096,480]{1,2,0:T(8,128)(2,1)S(1)} %get-tuple-element.7), kind=kOutput, calls=%fused_computation.17 | convolution fusion | flops 4039835136 | bytes 12060672 | tf_op jit(solution)/shard_map/pmk,ma->pka/dot_general | solution.py:66
  155.4 7.7 %all_to_all.26 = f32[4,1,512]{2,1,0:T(1,128)S(1)} all-to-all(f32[4,1,512]{2,1,0:T(1,128)S(1)} %broadcast_in_dim.8), channel_id=1, replica_groups=mesh['rows'=4,'grid_0'=8,'grid_1'=4,'grid_2'=2] {'rows'}, dimensions={0} | all-to-all | bytes 16384 | tf_op jit(solution)/shard_map/all_to_all | solution.py:36
  163.1 0.6 add_divide_fusion
  (4 shorter events, 0.1 us)
Async XLA Ops:
  6.5 57.8 %all-gather.4.cloned.1.call-start = ((), (), s32[]{:S(2)}) async-start(), calls=%async_computation.3 | async-start | bytes 2211840 | tf_op jit(solution)/shard_map/all_gather | solution.py:23
  20.9 62.3 %all-gather.6.cloned.1.call-start = ((), (), s32[]{:S(2)}) async-start(), calls=%async_computation.4 | async-start | bytes 5898240 | tf_op jit(solution)/shard_map/all_gather | solution.py:23
  65.6 24.5 %all-to-all-start.1 = ((s32[4,2,512]{2,1,0:T(2,128)}), s32[4,2,512]{2,1,0:T(2,128)S(1)}, u32[]{:S(2)}, u32[]{:S(2)}) async-start(s32[4,2,512]{2,1,0:T(2,128)} %broadcast_in_dim.7), calls=%async_computation.1 | async-start | bytes 32768 | tf_op jit(solution)/shard_map/all_to_all | solution.py:36
  90.1 5.1 %copy-start.1 = (s32[2,512]{1,0:T(2,128)S(1)}, s32[2,512]{1,0:T(2,128)}, u32[]{:S(2)}) copy-start(s32[2,512]{1,0:T(2,128)} %param.4) | copy-start | bytes 12292
  90.1 51.7 %all-to-all-start = ((bf16[2,512,1920]{1,0,2:T(2,128)(2,1)}), bf16[2,512,1920]{1,0,2:T(2,128)(2,1)}, u32[]{:S(2)}, u32[]{:S(2)}) async-start(bf16[2,512,1920]{1,0,2:T(2,128)(2,1)} %bitcast.38), calls=%async_computation | async-start | bytes 7864320 | tf_op jit(solution)/shard_map/all_to_all | solution.py:71
  149.6 1.6 copy-start
Sparse Core Ops, SparseCore 0:
  21.0 43.2 all-gather.3
  66.1 17.0 all-gather.5
where the time goes:
time: 171 us
  waiting for transfers between devices  84 us (49%)
  other arithmetic  21.4 us (13%)
  blocking collectives  20.2 us (12%)
  local copies, waits for them, and re-layouts  17.9 us (10%)
  between operations  13.5 us (8%)
  starting transfers between devices  9.4 us (5%)
  matrix products  4.22 us (2%)
    all_gather x2, waiting for transfers between devices, all_blocks(): pieces = lax.all_gather(pieces, axes[k], axis=0, tiled=True)  56.7 us
    all_to_all x1, waiting for transfers between devices, body(): lax.all_to_all(whole_columns, 'rows', split_axis=2, concat_axis=1, tiled=...  27.2 us
    another operation x1, other arithmetic  19.3 us
    all_gather x1, blocking collectives, all_blocks(): pieces = lax.all_gather(pieces, axes[k], axis=0, tiled=True)  12.5 us
    all_to_all x1, blocking collectives, from_everyone(): lax.all_to_all(jnp.broadcast_to(array[None], (devices, *array.shape)), ax...  7.66 us
    transpose x1, local copies, waits for them, and re-layouts, all_blocks(): pieces.transpose(*turned, *range(len(turns), pieces.ndim))  6.93 us
    all_to_all x1, starting transfers between devices, body(): lax.all_to_all(whole_columns, 'rows', split_axis=2, concat_axis=1, tiled=...  5.11 us
    all_to_all x1, starting transfers between devices, from_everyone(): lax.all_to_all(jnp.broadcast_to(array[None], (devices, *array.shape)), ax...  4.25 us
  transfers between devices with their start and end apart: 4, of which 3 were waited for; matrix products, arithmetic and copies ran while one was open for 16% of the time, Pallas kernels for 0%

commit v1 on v0

v1 whole, which is shorter than its diff:
```python
import jax
import jax.numpy as jnp
from jax import lax
from jax.sharding import Mesh
from jax.sharding import PartitionSpec as P

NOISE = 1920
PHASES = 4096
ROWS, FAR, NEAR, SIDE, CORE = "rows", "far", "near", "side", "core"
GRID = (FAR, NEAR, SIDE, CORE)


def sine_coefficients():
    import numpy as np

    nodes = 0.03125 * (1.0 - np.cos((np.arange(64) + 0.5) * np.pi / 64))
    root = np.sqrt(nodes)
    value = np.sin(2.0 * np.pi * root) / root
    return tuple(float(c) for c in np.polynomial.polynomial.polyfit(nodes, value, 5))


SINE = sine_coefficients()


def sine_of(u):
    square = u * u
    total = jnp.full_like(u, SINE[-1])
    for c in SINE[-2::-1]:
        total = total * square + c
    return total * u


def cos_sin_of(turns):
    rest = turns - jnp.round(turns)
    cos = sine_of(0.25 - jnp.abs(rest))
    sin = sine_of(jnp.maximum(jnp.minimum(rest, 0.5 - rest), -0.5 - rest))
    return cos, sin


def body(positions, angles, subspace):
    rows, far = lax.axis_size(ROWS), lax.axis_size(FAR)
    near, side = lax.axis_size(NEAR), lax.axis_size(SIDE)
    mine = jnp.concatenate([positions, angles], 0)
    lists = lax.all_to_all(
        jnp.broadcast_to(mine[None], (rows * far, *mine.shape)), (ROWS, FAR), 0, 0, tiled=True
    ).reshape(rows, far, *mine.shape)
    coords = jnp.moveaxis(lists[:, 0, :2], 1, 0).reshape(2, -1).astype(jnp.float32)
    turns = jnp.moveaxis(lists[0, :, 2:], 1, 0).reshape(2, -1).astype(jnp.float32) * (1.0 / PHASES)

    width = subspace.shape[2]
    quarter = -(-width // rows)
    columns = jnp.pad(subspace, ((0, 0), (0, 0), (0, rows * quarter - width)))
    columns = columns.reshape(2, -1, rows, quarter).transpose(2, 0, 3, 1)
    columns = columns.reshape(rows, 1, 2 * quarter, -1)
    pieces = jnp.broadcast_to(columns, (rows, near * side, *columns.shape[2:]))
    pieces = pieces.reshape(rows * near * side, *columns.shape[2:])
    got = lax.all_to_all(pieces, (ROWS, NEAR, SIDE), 0, 0, tiled=True)
    other = lax.ppermute(got, CORE, [(0, 1), (1, 0)])
    both = jnp.stack([got, other])
    both = both.reshape(2, rows, near * side, 2, quarter, -1)

    cos, sin = cos_sin_of(coords[0][:, None] * turns[0][None] + coords[1][:, None] * turns[1][None])
    steering = jnp.concatenate([cos.astype(jnp.bfloat16), sin.astype(jnp.bfloat16)], 1)
    weights = both.transpose(3, 0, 2, 4, 1, 5).reshape(-1, cos.shape[0])
    projected = jnp.dot(weights, steering, preferred_element_type=jnp.float32)
    projected = projected.reshape(2, -1, 2, cos.shape[1])
    real = projected[0, :, 0] + projected[1, :, 1]
    imag = projected[0, :, 1] - projected[1, :, 0]
    sums = jnp.sum(real * real + imag * imag, 0)

    sums = jnp.broadcast_to(sums.reshape(1, far, -1), (rows, far, sums.size // far))
    parts = lax.all_to_all(sums.reshape(rows * far, -1), (ROWS, FAR), 0, 0, tiled=True)
    return 1.0 / (jnp.sum(parts, 0) / NOISE + 1e-06)


def solution(mesh):
    split = Mesh(mesh.devices.reshape(mesh.shape["rows"], 4, 2, 4, 2), (ROWS, *GRID))
    in_specs = (P(None, ROWS), P(None, GRID), P(None, ROWS, GRID))
    return jax.shard_map(body, mesh=split, in_specs=in_specs, out_specs=P(GRID), check_vma=False)
```

time: 171 us -> 94.6 us (0.55)
  waiting for transfers between devices: 84 us -> 9.8 us
  other arithmetic: 21.4 us -> 39.9 us
  local copies, waits for them, and re-layouts: 17.9 us -> 2.59 us
  between operations: 13.5 us -> 0.09 us
  starting transfers between devices: 9.4 us -> 16.9 us
  matrix products: 4.22 us -> 10.1 us
  blocking collectives: 20.2 us -> 14.6 us
    all_gather x2 -> x0, waiting for transfers between devices: 56.7 us -> none  [all_blocks(): pieces = lax.all_gather(pieces, axes[k], axis=0, tiled=True)]
    convert_element_type x0 -> x2, other arithmetic: none -> 22.1 us  [the longest x1 22.1 us: body(): cos.astype(jnp.bfloat16)]
    another operation x2 -> x0, other arithmetic: 20.3 us -> none
    all_to_all x2, waiting for transfers between devices: 27.2 us -> 9.8 us  [the longest x1 9.8 us: body(): lax.all_to_all(jnp.broadcast_to(mine[None], (rows * far, *mine.shape)), (...]
    concatenate x0 -> x2, other arithmetic: none -> 14.5 us  [the longest x1 13.8 us: body(): jnp.concatenate([cos.astype(jnp.bfloat16), sin.astype(jnp.bfloat16)], 1)]
    all_gather x1 -> x0, blocking collectives: 12.5 us -> none  [all_blocks(): pieces = lax.all_gather(pieces, axes[k], axis=0, tiled=True)]
    all_to_all x2, starting transfers between devices: 9.35 us -> 16.9 us  [the longest x1 11 us: body(): lax.all_to_all(jnp.broadcast_to(mine[None], (rows * far, *mine.shape)), (...]
    all_to_all x1, blocking collectives: 7.66 us -> 14.6 us  [body(): lax.all_to_all(sums.reshape(rows * far, -1), (ROWS, FAR), 0, 0, tiled=True)]
  transfers between devices with their start and end apart: 4 -> 3, of which waited for: 3 -> 1; matrix products, arithmetic and copies ran while one was open for 16% -> 39% of each run, Pallas kernels for 0% -> 0%
where the time goes in v1:
time: 94.6 us; the launch traced here: 94 us
  other arithmetic  39.9 us (42%)
  starting transfers between devices  16.9 us (18%)
  blocking collectives  14.6 us (15%)
  matrix products  10.1 us (11%)
  waiting for transfers between devices  9.8 us (10%)
  local copies, waits for them, and re-layouts  2.59 us (3%)
    convert_element_type x1, other arithmetic, body(): cos.astype(jnp.bfloat16)  22.1 us
    all_to_all x1, blocking collectives, body(): lax.all_to_all(sums.reshape(rows * far, -1), (ROWS, FAR), 0, 0, tiled=True)  14.6 us
    concatenate x1, other arithmetic, body(): jnp.concatenate([cos.astype(jnp.bfloat16), sin.astype(jnp.bfloat16)], 1)  13.8 us
    all_to_all x1, starting transfers between devices, body(): lax.all_to_all(jnp.broadcast_to(mine[None], (rows * far, *mine.shape)), (...  11 us
    dot_general x1, matrix products, body(): projected = jnp.dot(weights, steering, preferred_element_type=jnp.float32)  10.1 us
    all_to_all x1, waiting for transfers between devices, body(): lax.all_to_all(jnp.broadcast_to(mine[None], (rows * far, *mine.shape)), (...  9.8 us
    all_to_all x1, starting transfers between devices, body(): got = lax.all_to_all(pieces, (ROWS, NEAR, SIDE), 0, 0, tiled=True)  5.9 us
    reduce_sum x1, other arithmetic, body(): sums = jnp.sum(real * real + imag * imag, 0)  2.53 us
  transfers between devices with their start and end apart: 3, of which 1 were waited for; matrix products, arithmetic and copies ran while one was open for 39% of the time, Pallas kernels for 0%

profile of v1, /device:TPU:8, one launch (start us, length us, event | category | flops | bytes accessed | tf_op | source)
XLA Modules:
  0.0 94.0 jit_solution(18208005587873275633)
XLA Ops:
  0.0 0.7 pad_add_fusion
  0.7 0.7 broadcast_in_dim.22
  1.4 11.0 %all-to-all-start.1 = ((s32[16,4,512]{2,1,0:T(4,128)}), s32[16,4,512]{2,1,0:T(4,128)S(1)}, u32[]{:S(2)}, u32[]{:S(2)}) async-start(s32[16,4,512]{2,1,0:T(4,128)} %broadcast_in_dim.22), calls=%async_computation.1 | async-start | bytes 262144 | tf_op jit(solution)/shard_map/all_to_all | solution.py:44
  12.4 0.8 copy.8
  13.3 9.8 %all-to-all-done.1 = s32[16,4,512]{2,1,0:T(4,128)S(1)} async-done(((s32[16,4,512]{2,1,0:T(4,128)}), s32[16,4,512]{2,1,0:T(4,128)S(1)}, u32[]{:S(2)}, u32[]{:S(2)}) %all-to-all-start.1) | async-done | bytes 131104 | tf_op jit(solution)/shard_map/all_to_all | solution.py:44
  23.1 0.9 broadcast_in_dim.21
  23.9 5.9 %all-to-all-start = ((bf16[32,16,512]{2,1,0:T(8,128)(2,1)}), bf16[32,16,512]{2,1,0:T(8,128)(2,1)S(1)}, u32[]{:S(2)}, u32[]{:S(2)}) async-start(bf16[32,16,512]{2,1,0:T(8,128)(2,1)} %bitcast.3), calls=%async_computation | async-start | bytes 1048576 | tf_op jit(solution)/shard_map/all_to_all | solution.py:57
  29.9 22.1 %multiply_convert_fusion.1 = (bf16[2048,2048]{0,1:T(8,128)(2,1)}, bf16[2048,2048]{0,1:T(8,128)(2,1)}) fusion(f32[2048]{0:T(1024)S(1)} %bitcast.46, f32[2048]{0:T(1024)S(1)} %bitcast.44, f32[2048]{0:T(1024)S(1)} %bitcast.45, f32[2048]{0:T(1024)S(1)} %bitcast.43), kind=kLoop, calls=%fused_computation.11 | loop fusion | flops 155189248 | bytes 16809984 | tf_op jit(solution)/shard_map/convert_element_type | solution.py:63
  52.0 0.0 all-to-all-done
  52.0 0.0 collective-permute-start
  52.0 13.8 %pad_maximum_fusion = bf16[2048,4096]{0,1:T(8,128)(2,1)} fusion(bf16[2048,2048]{0,1:T(8,128)(2,1)} %get-tuple-element.6, bf16[2048,2048]{0,1:T(8,128)(2,1)} %get-tuple-element.5), kind=kLoop, calls=%fused_computation.3 | loop fusion | flops 33554432 | bytes 33554432 | tf_op jit(solution)/shard_map/concatenate | solution.py:63
  65.8 0.0 collective-permute-done
  65.8 0.1 maximum_bitcast_fusion
  65.9 0.1 copy.10
  66.1 10.1 %fusion.16 = f32[2,128,2,2048]{3,1,2,0:T(8,128)} fusion(bf16[2,128,2048,1]{2,1,3,0:T(8,128)(2,1)S(1)} %bitcast.39, bf16[2,2048,2048,1]{2,1,0,3:T(8,128)(2,1)} %bitcast.37), kind=kOutput, calls=%fused_computation.36 | convolution fusion | flops 4294967296 | bytes 22020096 | tf_op jit(solution)/shard_map/dot_general | solution.py:65
  76.1 2.5 %fusion.9 = f32[2048]{0:T(1024)S(1)} fusion(f32[2,128,2,2048]{3,1,2,0:T(8,128)} %fusion.16), kind=kLoop, calls=%fused_computation.21 | loop fusion | flops 1570816 | bytes 4202496 | tf_op jit(solution)/shard_map/reduce_sum | solution.py:69
  78.7 0.1 all_to_all.14
  78.8 14.6 %all_to_all.19 = f32[16,1,512]{2,1,0:T(1,128)S(1)} all-to-all(f32[16,1,512]{2,1,0:T(1,128)S(1)} %all_to_all.14), channel_id=1, replica_groups=mesh['rows'=4,'far'=4,'near'=2,'side'=4,'core'=2] {'rows','far'}, dimensions={0} | all-to-all | bytes 65536 | tf_op jit(solution)/shard_map/all_to_all | solution.py:72
  93.4 0.6 add_divide_fusion
  (8 shorter events, 0.1 us)
Async XLA Ops:
  1.4 21.7 %all-to-all-start.1 = ((s32[16,4,512]{2,1,0:T(4,128)}), s32[16,4,512]{2,1,0:T(4,128)S(1)}, u32[]{:S(2)}, u32[]{:S(2)}) async-start(s32[16,4,512]{2,1,0:T(4,128)} %broadcast_in_dim.22), calls=%async_computation.1 | async-start | bytes 262144 | tf_op jit(solution)/shard_map/all_to_all | solution.py:44
  23.9 28.1 %all-to-all-start = ((bf16[32,16,512]{2,1,0:T(8,128)(2,1)}), bf16[32,16,512]{2,1,0:T(8,128)(2,1)S(1)}, u32[]{:S(2)}, u32[]{:S(2)}) async-start(bf16[32,16,512]{2,1,0:T(8,128)(2,1)} %bitcast.3), calls=%async_computation | async-start | bytes 1048576 | tf_op jit(solution)/shard_map/all_to_all | solution.py:57
  52.0 13.8 %collective-permute-start = (bf16[32,16,512]{2,1,0:T(8,128)(2,1)S(1)}, bf16[32,16,512]{2,1,0:T(8,128)(2,1)S(1)}, u32[]{:S(2)}, u32[]{:S(2)}) collective-permute-start(bf16[32,16,512]{2,1,0:T(8,128)(2,1)S(1)} %all-to-all-done), channel_id=1, source_target_pairs={{0,1},{1,0},{2,3},{3,2},{4,5},{5,4},{6,7},{7,6},{8,9},{9,8},{10,11... | collective-permute-start | bytes 1572872 | tf_op jit(solution)/shard_map/ppermute | solution.py:58

commit v2 on v1

v2 whole, which is shorter than its diff:
```python
import jax
import jax.numpy as jnp
import numpy as np
from jax import lax
from jax.experimental import pallas as pl
from jax.experimental.pallas import tpu as pltpu
from jax.sharding import Mesh
from jax.sharding import PartitionSpec as P

NOISE = 1920
PHASES = 4096
LATTICE = 64
LANES = 128
BATCH = 32
PITCH = 36
ROWS, FAR, NEAR, SIDE, CORE = "rows", "far", "near", "side", "core"
GRID = (FAR, NEAR, SIDE, CORE)


def sine_coefficients():
    nodes = 0.03125 * (1.0 - np.cos((np.arange(64) + 0.5) * np.pi / 64))
    root = np.sqrt(nodes)
    value = np.sin(2.0 * np.pi * root) / root
    return tuple(float(c) for c in np.polynomial.polynomial.polyfit(nodes, value, 5))


SINE = sine_coefficients()


def sine_of(u):
    square = u * u
    total = jnp.full_like(u, SINE[-1])
    for c in SINE[-2::-1]:
        total = total * square + c
    return total * u


def cos_sin_of(turns):
    rest = turns - jnp.round(turns)
    cos = sine_of(0.25 - jnp.abs(rest))
    sin = sine_of(jnp.maximum(jnp.minimum(rest, 0.5 - rest), -0.5 - rest))
    return cos, sin


def steering_kernel(rows_ref, turns_ref, out_ref, table, stage):
    blocks = turns_ref.shape[1]

    def fill(step, carry):
        for k in range(2):
            cos, sin = cos_sin_of(turns_ref[k] * step.astype(jnp.float32))
            here = pl.ds(pl.multiple_of(step * blocks, blocks), blocks)
            table[2 * k, here, :] = cos
            table[2 * k + 1, here, :] = sin
        return carry

    lax.fori_loop(0, LATTICE, fill, 0, unroll=4)

    def batch(step, carry):
        first = pl.multiple_of(step * BATCH, BATCH)
        for e in range(BATCH):
            one = pl.ds(pl.multiple_of(rows_ref[0, first + e], blocks), blocks)
            two = pl.ds(pl.multiple_of(rows_ref[1, first + e], blocks), blocks)
            cos_one, sin_one = table[0, one, :], table[1, one, :]
            cos_two, sin_two = table[2, two, :], table[3, two, :]
            stage[0, pl.ds(e, blocks, stride=PITCH), :] = cos_one * cos_two - sin_one * sin_two
            stage[1, pl.ds(e, blocks, stride=PITCH), :] = sin_one * cos_two + cos_one * sin_two
        for k in range(2):
            for b in range(blocks):
                part = stage[k, b * PITCH : b * PITCH + BATCH, :]
                out_ref[k, b, pl.ds(first, BATCH), :] = part.astype(out_ref.dtype)
        return carry

    lax.fori_loop(0, out_ref.shape[2] // BATCH, batch, 0)


def steering_of(table_rows, turns):
    blocks, elements = turns.shape[1], table_rows.shape[1]
    return pl.pallas_call(
        steering_kernel,
        out_shape=pltpu.VMEM((2, blocks, elements, LANES), jnp.bfloat16),
        in_specs=[
            pl.BlockSpec(memory_space=pltpu.SMEM),
            pl.BlockSpec(memory_space=pltpu.VMEM),
        ],
        out_specs=pl.BlockSpec(memory_space=pltpu.VMEM),
        scratch_shapes=[
            pltpu.VMEM((4, LATTICE * blocks, LANES), jnp.float32),
            pltpu.VMEM((2, blocks * PITCH, LANES), jnp.float32),
        ],
        cost_estimate=pl.CostEstimate(
            flops=6 * blocks * elements * LANES, bytes_accessed=0, transcendentals=0
        ),
        compiler_params=pltpu.CompilerParams(vmem_limit_bytes=24 * 2**20),
        name="steering",
    )(table_rows, turns)


def sums_kernel(own_ref, other_ref, steering_ref, out_ref):
    weights = [
        jnp.concatenate([ref[r] for r in range(ref.shape[0])], 1) for ref in (own_ref, other_ref)
    ]
    weights = jnp.concatenate(weights, 0)
    for b in range(steering_ref.shape[1]):
        both = jnp.concatenate([steering_ref[0, b], steering_ref[1, b]], 1)
        product = jnp.dot(weights, both, preferred_element_type=jnp.float32)
        total = jnp.zeros((8, LANES), jnp.float32)
        for g in range(0, product.shape[0], 16):
            upper, lower = product[g : g + 8], product[g + 8 : g + 16]
            real = upper[:, :LANES] + lower[:, LANES:]
            imag = upper[:, LANES:] - lower[:, :LANES]
            total = total + (real * real + imag * imag)
        out_ref[b : b + 1, :] = jnp.sum(total, 0, keepdims=True)


def sums_of(own, other, steering):
    blocks = steering.shape[1]
    return pl.pallas_call(
        sums_kernel,
        out_shape=jax.ShapeDtypeStruct((blocks, LANES), jnp.float32),
        in_specs=[pl.BlockSpec(memory_space=pltpu.VMEM)] * 3,
        out_specs=pl.BlockSpec(memory_space=pltpu.VMEM),
        cost_estimate=pl.CostEstimate(
            flops=8 * own.shape[1] * own.shape[0] * own.shape[2] * blocks * LANES,
            bytes_accessed=0,
            transcendentals=0,
        ),
        compiler_params=pltpu.CompilerParams(vmem_limit_bytes=24 * 2**20),
        name="sums",
    )(own, other, steering)


def body(positions, angles, subspace):
    rows, far = lax.axis_size(ROWS), lax.axis_size(FAR)
    near, side = lax.axis_size(NEAR), lax.axis_size(SIDE)
    mine = jnp.concatenate([positions, angles], 0)
    lists = lax.all_to_all(
        jnp.broadcast_to(mine[None], (rows * far, *mine.shape)), (ROWS, FAR), 0, 0, tiled=True
    ).reshape(rows, far, *mine.shape)
    blocks = far * angles.shape[1] // LANES
    table_rows = jnp.moveaxis(lists[:, 0, :2], 1, 0).reshape(2, -1) * blocks
    turns = jnp.moveaxis(lists[0, :, 2:], 1, 0).reshape(2, blocks, LANES)
    steering = steering_of(table_rows, turns.astype(jnp.float32) * (1.0 / PHASES))

    width = subspace.shape[2]
    quarter = -(-width // rows)
    columns = jnp.pad(subspace, ((0, 0), (0, 0), (0, rows * quarter - width)))
    columns = columns.reshape(2, -1, rows, quarter).transpose(2, 0, 3, 1)
    columns = columns.reshape(rows, 1, 2 * quarter, -1)
    pieces = jnp.broadcast_to(columns, (rows, near * side, *columns.shape[2:]))
    pieces = pieces.reshape(rows * near * side, *columns.shape[2:])
    own = lax.all_to_all(pieces, (ROWS, NEAR, SIDE), 0, 0, tiled=True)
    other = lax.ppermute(own, CORE, [(0, 1), (1, 0)])
    own, other = (part.reshape(rows, -1, part.shape[2]) for part in (own, other))

    sums = sums_of(own, other, steering).reshape(1, far, -1)
    sums = jnp.broadcast_to(sums, (rows, *sums.shape[1:]))
    parts = lax.all_to_all(sums.reshape(rows * far, -1), (ROWS, FAR), 0, 0, tiled=True)
    return 1.0 / (jnp.sum(parts, 0) / NOISE + 1e-06)


def solution(mesh):
    split = Mesh(mesh.devices.reshape(mesh.shape["rows"], 4, 2, 4, 2), (ROWS, *GRID))
    in_specs = (P(None, ROWS), P(None, GRID), P(None, ROWS, GRID))
    return jax.shard_map(body, mesh=split, in_specs=in_specs, out_specs=P(GRID), check_vma=False)
```

time: 94.6 us -> 71.4 us (0.75)
  other arithmetic: 39.9 us -> 1.37 us
  Pallas kernels: 0 us -> 16.3 us
  waiting for transfers between devices: 9.8 us -> 20.6 us
  matrix products: 10.1 us -> 0 us
  blocking collectives: 14.6 us -> 12.7 us
    convert_element_type x2 -> x0, other arithmetic: 22.1 us -> none  [the longest x1 22.1 us: body(): cos.astype(jnp.bfloat16)]
    pallas_call x0 -> x2, Pallas kernels: none -> 16.3 us  [the longest x1 11.8 us: steering_of(): pl.pallas_call(steering_kernel, out_shape=pltpu.VMEM((2, blocks, elements...]
    concatenate x1 -> x0, other arithmetic: 13.8 us -> none  [body(): jnp.concatenate([cos.astype(jnp.bfloat16), sin.astype(jnp.bfloat16)], 1)]
    dot_general x1 -> x0, matrix products: 10.1 us -> none  [body(): projected = jnp.dot(weights, steering, preferred_element_type=jnp.float32)]
    all_to_all x1, waiting for transfers between devices: 0.01 us -> 10 us  [body(): own = lax.all_to_all(pieces, (ROWS, NEAR, SIDE), 0, 0, tiled=True)]
    all_to_all x1, starting transfers between devices: 5.9 us -> 8.89 us  [body(): own = lax.all_to_all(pieces, (ROWS, NEAR, SIDE), 0, 0, tiled=True)]
    reduce_sum x1 -> x0, other arithmetic: 2.53 us -> none  [body(): sums = jnp.sum(real * real + imag * imag, 0)]
    all_to_all x1, starting transfers between devices: 11 us -> 8.51 us  [body(): lax.all_to_all(jnp.broadcast_to(mine[None], (rows * far, *mine.shape)), (...]
  transfers between devices with their start and end apart: 3 -> 3, of which waited for: 1 -> 2; matrix products, arithmetic and copies ran while one was open for 39% -> 1% of each run, Pallas kernels for 0% -> 17%
where the time goes in v2:
time: 71.4 us; the launch traced here: 71 us
  waiting for transfers between devices  20.6 us (29%)
  starting transfers between devices  17.5 us (25%)
  Pallas kernels  16.3 us (23%)
  blocking collectives  12.7 us (18%)
  local copies, waits for them, and re-layouts  2.45 us (3%)
  other arithmetic  1.37 us (2%)
    all_to_all x1, blocking collectives, body(): lax.all_to_all(sums.reshape(rows * far, -1), (ROWS, FAR), 0, 0, tiled=True)  12.7 us
    pallas_call x1, Pallas kernels, steering_of(): pl.pallas_call(steering_kernel, out_shape=pltpu.VMEM((2, blocks, elements...  11.8 us
    all_to_all x1, waiting for transfers between devices, body(): lax.all_to_all(jnp.broadcast_to(mine[None], (rows * far, *mine.shape)), (...  10.6 us
    all_to_all x1, waiting for transfers between devices, body(): own = lax.all_to_all(pieces, (ROWS, NEAR, SIDE), 0, 0, tiled=True)  10 us
    all_to_all x1, starting transfers between devices, body(): own = lax.all_to_all(pieces, (ROWS, NEAR, SIDE), 0, 0, tiled=True)  8.89 us
    all_to_all x1, starting transfers between devices, body(): lax.all_to_all(jnp.broadcast_to(mine[None], (rows * far, *mine.shape)), (...  8.51 us
    pallas_call x1, Pallas kernels, sums_of(): pl.pallas_call(sums_kernel, out_shape=jax.ShapeDtypeStruct((blocks, LANES...  4.5 us
  transfers between devices with their start and end apart: 3, of which 2 were waited for; matrix products, arithmetic and copies ran while one was open for 1% of the time, Pallas kernels for 17%

profile of v2, /device:TPU:8, one launch (start us, length us, event | category | flops | bytes accessed | tf_op | source)
XLA Modules:
  0.0 71.0 jit_solution(8915585679208891665)
XLA Ops:
  0.0 0.8 %copy.8 = bf16[2,512,30]{1,2,0:T(8,128)(2,1)S(1)} copy(bf16[2,512,30]{1,0,2:T(2,128)(2,1)} %param.5) | data formatting | bytes 122880 | tf_op args[2]
  0.9 0.9 %broadcast_in_dim.21 = bf16[4,8,16,512]{3,2,1,0:T(8,128)(2,1)} broadcast(bf16[4,16,512]{2,1,0:T(8,128)(2,1)S(1)} %copy_bitcast_fusion), dimensions={0,2,3} | broadcast | bytes 589824 | tf_op jit(solution)/shard_map/broadcast_in_dim | solution.py:149
  1.7 8.9 %all-to-all-start = ((bf16[32,16,512]{2,1,0:T(8,128)(2,1)}), bf16[32,16,512]{2,1,0:T(8,128)(2,1)S(1)}, u32[]{:S(2)}, u32[]{:S(2)}) async-start(bf16[32,16,512]{2,1,0:T(8,128)(2,1)} %bitcast.3), calls=%async_computation | async-start | bytes 1048576 | tf_op jit(solution)/shard_map/all_to_all | solution.py:151
  10.6 0.7 %pad_add_fusion = s32[4,512]{1,0:T(4,128)S(1)} fusion(s32[2,512]{1,0:T(2,128)} %param.4, s32[2,512]{1,0:T(2,128)} %param.3), kind=kLoop, calls=%fused_computation.6 | loop fusion | flops 2048 | bytes 16384 | tf_op jit(solution)/shard_map/concatenate | solution.py:135
  11.3 10.0 %all-to-all-done = bf16[32,16,512]{2,1,0:T(8,128)(2,1)S(1)} async-done(((bf16[32,16,512]{2,1,0:T(8,128)(2,1)}), bf16[32,16,512]{2,1,0:T(8,128)(2,1)S(1)}, u32[]{:S(2)}, u32[]{:S(2)}) %all-to-all-start) | async-done | bytes 524320 | tf_op jit(solution)/shard_map/all_to_all | solution.py:151
  21.3 0.7 broadcast_in_dim.22
  22.0 8.5 %all-to-all-start.1 = ((s32[16,4,512]{2,1,0:T(4,128)}), s32[16,4,512]{2,1,0:T(4,128)S(1)}, u32[]{:S(2)}, u32[]{:S(2)}) async-start(s32[16,4,512]{2,1,0:T(4,128)} %broadcast_in_dim.22), calls=%async_computation.1 | async-start | bytes 262144 | tf_op jit(solution)/shard_map/all_to_all | solution.py:136
  30.5 0.1 collective-permute-start
  30.6 10.6 %all-to-all-done.1 = s32[16,4,512]{2,1,0:T(4,128)S(1)} async-done(((s32[16,4,512]{2,1,0:T(4,128)}), s32[16,4,512]{2,1,0:T(4,128)S(1)}, u32[]{:S(2)}, u32[]{:S(2)}) %all-to-all-start.1) | async-done | bytes 131104 | tf_op jit(solution)/shard_map/all_to_all | solution.py:136
  41.2 11.8 %steering.1.steering_ref = bf16[2,16,2048,128]{3,2,1,0:T(8,128)(2,1)S(1)} custom-call(s32[2,2048]{1,0:T(2,128)S(1)} %bitcast.22, f32[2,16,128]{2,1,0:T(8,128)S(1)} %mul.33.turns_ref), custom_call_target="tpu_custom_call" | custom-call | flops 25165824 | tf_op jit(solution)/shard_map/steering/pallas_call | solution.py:78
  53.1 0.0 collective-permute-done
  53.1 4.5 %sums.1 = f32[16,128]{1,0:T(8,128)S(1)} custom-call(bf16[4,128,512]{2,1,0:T(8,128)(2,1)S(1)} %bitcast.20, bf16[4,128,512]{2,1,0:T(8,128)(2,1)S(1)} %bitcast.21, bf16[2,16,2048,128]{3,2,1,0:T(8,128)(2,1)S(1)} %steering.1.steering_ref), custom_call_target="tpu_custom_call" | custom-call | flops 4294967296 | tf_op jit(solution)/shard_map/sums/pallas_call | solution.py:117
  57.6 0.1 all_to_all.14
  57.7 12.7 %all_to_all.19 = f32[16,1,512]{2,1,0:T(1,128)S(1)} all-to-all(f32[16,1,512]{2,1,0:T(1,128)S(1)} %all_to_all.14), channel_id=1, replica_groups=mesh['rows'=4,'far'=4,'near'=2,'side'=4,'core'=2] {'rows','far'}, dimensions={0} | all-to-all | bytes 65536 | tf_op jit(solution)/shard_map/all_to_all | solution.py:157
  70.4 0.6 add_divide_fusion
  (8 shorter events, 0.1 us)
Async XLA Ops:
  1.7 19.6 %all-to-all-start = ((bf16[32,16,512]{2,1,0:T(8,128)(2,1)}), bf16[32,16,512]{2,1,0:T(8,128)(2,1)S(1)}, u32[]{:S(2)}, u32[]{:S(2)}) async-start(bf16[32,16,512]{2,1,0:T(8,128)(2,1)} %bitcast.3), calls=%async_computation | async-start | bytes 1048576 | tf_op jit(solution)/shard_map/all_to_all | solution.py:151
  22.0 19.2 %all-to-all-start.1 = ((s32[16,4,512]{2,1,0:T(4,128)}), s32[16,4,512]{2,1,0:T(4,128)S(1)}, u32[]{:S(2)}, u32[]{:S(2)}) async-start(s32[16,4,512]{2,1,0:T(4,128)} %broadcast_in_dim.22), calls=%async_computation.1 | async-start | bytes 262144 | tf_op jit(solution)/shard_map/all_to_all | solution.py:136
  30.5 22.6 %collective-permute-start = (bf16[32,16,512]{2,1,0:T(8,128)(2,1)S(1)}, bf16[32,16,512]{2,1,0:T(8,128)(2,1)S(1)}, u32[]{:S(2)}, u32[]{:S(2)}) collective-permute-start(bf16[32,16,512]{2,1,0:T(8,128)(2,1)S(1)} %all-to-all-done), channel_id=1, source_target_pairs={{0,1},{1,0},{2,3},{3,2},{4,5},{5,4},{6,7},{7,6},{8,9},{9,8},{10,11... | collective-permute-start | bytes 1572872 | tf_op jit(solution)/shard_map/ppermute | solution.py:152

commit v3 on v1

v3 whole, which is shorter than its diff:
```python
import jax
import jax.numpy as jnp
import numpy as np
from jax import lax
from jax.experimental import pallas as pl
from jax.experimental.pallas import tpu as pltpu
from jax.sharding import Mesh
from jax.sharding import PartitionSpec as P

NOISE = 1920
PHASES = 4096
LATTICE = 64
DIGIT = 6
LANES = 128
BATCH = 32
EXTRA = 4
ROWS, DEEP, SIDE, CORE = "rows", "deep", "side", "core"
GRID = (DEEP, SIDE, CORE)


def sine_coefficients():
    nodes = 0.03125 * (1.0 - np.cos((np.arange(64) + 0.5) * np.pi / 64))
    root = np.sqrt(nodes)
    value = np.sin(2.0 * np.pi * root) / root
    return tuple(float(c) for c in np.polynomial.polynomial.polyfit(nodes, value, 5))


SINE = sine_coefficients()


def sine_of(u):
    square = u * u
    total = jnp.full_like(u, SINE[-1])
    for c in SINE[-2::-1]:
        total = total * square + c
    return total * u


def cos_sin_of(turns):
    rest = turns - jnp.round(turns)
    cos = sine_of(0.25 - jnp.abs(rest))
    sin = sine_of(jnp.maximum(jnp.minimum(rest, 0.5 - rest), -0.5 - rest))
    return cos, sin


def pack_kernel(positions_ref, angles_ref, columns_ref, out_ref):
    group, pairs, _, share = out_ref.shape
    each, width = pairs - 3, columns_ref.shape[0]
    angles = angles_ref[...]
    lists = (positions_ref[...], angles >> DIGIT, angles & (LATTICE - 1))
    lists = [part.astype(jnp.float32).astype(out_ref.dtype) for part in lists]
    for g in range(group):
        for c in range(each):
            if g * each + c < width:
                out_ref[g, c] = columns_ref[g * each + c]
            else:
                out_ref[g, c] = jnp.zeros((2, share), out_ref.dtype)
        for k in range(3):
            out_ref[g, each + k] = lists[k]


def packed(positions, angles, columns, group):
    width, _, share = columns.shape
    pairs = -(-width // group) + 3
    return pl.pallas_call(
        pack_kernel,
        out_shape=jax.ShapeDtypeStruct((group, pairs, 2, share), columns.dtype),
        in_specs=[pl.BlockSpec(memory_space=pltpu.VMEM)] * 3,
        out_specs=pl.BlockSpec(memory_space=pltpu.VMEM),
        cost_estimate=pl.CostEstimate(flops=2**16, bytes_accessed=0, transcendentals=0),
        name="pack",
    )(positions, angles, columns)


def rows_kernel(lists_ref, rows_ref):
    row_groups, side, pairs, _, share = lists_ref.shape
    scale = 2 * side * share // LANES
    for r in range(row_groups):
        coordinates = lists_ref[r, 0, pairs - 3].astype(jnp.float32) * scale
        rows_ref[:, r * share : (r + 1) * share] = coordinates.astype(jnp.int32)


def tables_kernel(lists_ref, table_ref, turns):
    _, side, pairs, _, share = lists_ref.shape
    blocks = turns.shape[1]
    for s in range(side):
        high = lists_ref[0, s, pairs - 2].astype(jnp.float32)
        low = lists_ref[0, s, pairs - 1].astype(jnp.float32)
        part = high * (LATTICE / PHASES) + low * (1.0 / PHASES)
        for j in range(share // LANES):
            b = s * (share // LANES) + j
            for k in range(2):
                turns[k, b : b + 1, :] = part[k : k + 1, j * LANES : (j + 1) * LANES]

    def fill(step, carry):
        for k in range(2):
            cos, sin = cos_sin_of(turns[k] * step.astype(jnp.float32))
            first = pl.multiple_of(2 * step * blocks, 2 * blocks)
            table_ref[k, pl.ds(first, blocks), :] = cos
            table_ref[k, pl.ds(first + blocks, blocks), :] = sin
        return carry

    lax.fori_loop(0, LATTICE, fill, 0, unroll=4)


def tables_of(lists):
    row_groups, side, _, _, share = lists.shape
    blocks = side * share // LANES
    rows = pl.pallas_call(
        rows_kernel,
        out_shape=pltpu.VMEM((2, row_groups * share), jnp.int32),
        in_specs=[pl.BlockSpec(memory_space=pltpu.VMEM)],
        out_specs=pl.BlockSpec(memory_space=pltpu.VMEM),
        name="rows",
    )(lists)
    table = pl.pallas_call(
        tables_kernel,
        out_shape=pltpu.VMEM((2, LATTICE * 2 * blocks, LANES), jnp.float32),
        in_specs=[pl.BlockSpec(memory_space=pltpu.VMEM)],
        out_specs=pl.BlockSpec(memory_space=pltpu.VMEM),
        scratch_shapes=[pltpu.VMEM((2, blocks, LANES), jnp.float32)],
        cost_estimate=pl.CostEstimate(flops=2**22, bytes_accessed=0, transcendentals=0),
        compiler_params=pltpu.CompilerParams(vmem_limit_bytes=4 * 2**20),
        name="tables",
    )(lists)
    return table, rows


def sums_kernel(rows_ref, table_ref, own_ref, other_ref, out_ref, steering):
    deep, row_groups, _, _, share = own_ref.shape
    blocks, elements = out_ref.shape[0], row_groups * share
    pitch = elements + EXTRA

    def batch(step, carry):
        first = pl.multiple_of(step * BATCH, BATCH)
        for e in range(BATCH):
            one = pl.multiple_of(rows_ref[0, first + e], 2 * blocks)
            two = pl.multiple_of(rows_ref[1, first + e], 2 * blocks)
            cos_one, sin_one = jnp.split(table_ref[0, pl.ds(one, 2 * blocks), :], 2)
            cos_two, sin_two = jnp.split(table_ref[1, pl.ds(two, 2 * blocks), :], 2)
            here = pl.ds(first + e, blocks, stride=pitch)
            steering[0, here, :] = cos_one * cos_two - sin_one * sin_two
            steering[1, here, :] = sin_one * cos_two + cos_one * sin_two
        return carry

    lax.fori_loop(0, elements // BATCH, batch, 0)

    weights = jnp.concatenate(
        [
            jnp.concatenate([ref[d, r].reshape(-1, share) for r in range(row_groups)], 1)
            for ref in (own_ref, other_ref)
            for d in range(deep)
        ],
        0,
    )
    is_real = lax.broadcasted_iota(jnp.int32, (8, LANES), 0) % 2 == 0
    for b in range(blocks):
        both = [
            steering[k, b * pitch : b * pitch + elements, :].astype(weights.dtype) for k in range(2)
        ]
        both = jnp.concatenate(both, 1)
        product = jnp.dot(weights, both, preferred_element_type=jnp.float32)
        total = jnp.zeros((8, LANES), jnp.float32)
        for g in range(0, product.shape[0], 8):
            cos, sin = product[g : g + 8, :LANES], product[g : g + 8, LANES:]
            real = cos + pltpu.roll(sin, 7, 0)
            imag = sin - pltpu.roll(cos, 7, 0)
            total = total + (real * real + imag * imag)
        out_ref[b : b + 1, :] = jnp.sum(jnp.where(is_real, total, 0.0), 0, keepdims=True)


def sums_of(table, rows, own, other):
    blocks = table.shape[1] // (2 * LATTICE)
    return pl.pallas_call(
        sums_kernel,
        out_shape=jax.ShapeDtypeStruct((blocks, LANES), jnp.float32),
        in_specs=[pl.BlockSpec(memory_space=pltpu.SMEM)]
        + [pl.BlockSpec(memory_space=pltpu.VMEM)] * 3,
        out_specs=pl.BlockSpec(memory_space=pltpu.VMEM),
        scratch_shapes=[pltpu.VMEM((2, blocks * (rows.shape[1] + EXTRA), LANES), jnp.float32)],
        cost_estimate=pl.CostEstimate(
            flops=8 * own.size * blocks * LANES, bytes_accessed=0, transcendentals=0
        ),
        compiler_params=pltpu.CompilerParams(vmem_limit_bytes=44 * 2**20),
        name="sums",
    )(rows, table, own, other)


def body(positions, angles, subspace):
    rows, side, deep = lax.axis_size(ROWS), lax.axis_size(SIDE), lax.axis_size(DEEP)
    group = rows * side
    share, width = subspace.shape[1:]
    each = -(-width // group)
    pieces = packed(positions, angles, subspace.transpose(2, 0, 1), group)
    got = lax.all_to_all(pieces, (ROWS, SIDE), 0, 0, tiled=True)
    got = got.reshape(rows, side, *pieces.shape[1:])

    columns = got[:, :, :each].reshape(1, rows, side * each, 2, share)
    columns = jnp.broadcast_to(columns, (deep, *columns.shape[1:]))
    own = lax.all_to_all(columns, DEEP, 0, 0, tiled=True)
    other = lax.ppermute(own, CORE, [(0, 1), (1, 0)])

    table, table_rows = tables_of(got)
    sums = sums_of(table, table_rows, own, other).reshape(1, side, -1)
    sums = jnp.broadcast_to(sums, (rows, *sums.shape[1:]))
    parts = lax.all_to_all(sums.reshape(group, -1), (ROWS, SIDE), 0, 0, tiled=True)
    return 1.0 / (jnp.sum(parts, 0) / NOISE + 1e-06)


def solution(mesh):
    split = Mesh(mesh.devices.reshape(mesh.shape["rows"], 8, 4, 2), (ROWS, *GRID))
    in_specs = (P(None, ROWS), P(None, GRID), P(None, ROWS, GRID))
    return jax.shard_map(body, mesh=split, in_specs=in_specs, out_specs=P(GRID), check_vma=False)
```

time: 94.6 us -> 69.3 us (0.73)
  the two profiles are of different devices: /device:TPU:8 before, /device:TPU:1 now
where the time goes in v3:
time: 69.3 us; the launch traced here: 69 us
  blocking collectives  47 us (68%)
  Pallas kernels  16.1 us (23%)
  starting transfers between devices  3.74 us (5%)
  local copies, waits for them, and re-layouts  1.5 us (2%)
    all_to_all x1, blocking collectives, body(): own = lax.all_to_all(columns, DEEP, 0, 0, tiled=True)  22.7 us
    all_to_all x1, blocking collectives, body(): got = lax.all_to_all(pieces, (ROWS, SIDE), 0, 0, tiled=True)  14.6 us
    pallas_call x1, Pallas kernels, sums_of(): pl.pallas_call(sums_kernel, out_shape=jax.ShapeDtypeStruct((blocks, LANES...  12.3 us
    all_to_all x1, blocking collectives, body(): lax.all_to_all(sums.reshape(group, -1), (ROWS, SIDE), 0, 0, tiled=True)  9.76 us
    ppermute x1, starting transfers between devices, body(): other = lax.ppermute(own, CORE, [(0, 1), (1, 0)])  3.74 us
    pallas_call x1, Pallas kernels, packed(): pl.pallas_call(pack_kernel, out_shape=jax.ShapeDtypeStruct((group, pairs,...  1.55 us
  transfers between devices with their start and end apart: 1, of which 0 were waited for; matrix products, arithmetic and copies ran while one was open for 0% of the time, Pallas kernels for 3%

profile of v3, /device:TPU:1, one launch (start us, length us, event | category | flops | bytes accessed | tf_op | source)
XLA Modules:
  0.0 69.0 jit_solution(12776678599317189888)
XLA Ops:
  0.0 1.6 %pack.1 = bf16[16,5,2,512]{3,2,1,0:T(2,128)(2,1)} custom-call(s32[2,512]{1,0:T(2,128)} %positions_ref.1, s32[2,512]{1,0:T(2,128)} %angles_ref.1, bf16[30,2,512]{2,1,0:T(2,128)(2,1)} %bitcast.7), custom_call_target="tpu_custom_call" | custom-call | flops 65536 | tf_op jit(solution)/shard_map/pack/pallas_call | solution.py:65
  1.6 14.6 %all_to_all.19 = bf16[16,5,2,512]{3,2,1,0:T(2,128)(2,1)S(1)} all-to-all(bf16[16,5,2,512]{3,2,1,0:T(2,128)(2,1)} %pack.1), channel_id=1, replica_groups=mesh['rows'=4,'deep'=8,'side'=4,'core'=2] {'rows','side'}, dimensions={0} | all-to-all | bytes 327680 | tf_op jit(solution)/shard_map/all_to_all | solution.py:195
  16.1 0.0 copy-start
  16.2 0.5 broadcast_in_dim.15
  16.6 22.7 %all_to_all.20.own_ref = bf16[8,4,8,2,512]{4,3,2,1,0:T(2,128)(2,1)S(1)} all-to-all(bf16[8,4,8,2,512]{4,3,2,1,0:T(2,128)(2,1)S(1)} %broadcast_in_dim.15), channel_id=1, replica_groups=mesh['rows'=4,'deep'=8,'side'=4,'core'=2] {'deep'}, dimensions={0} | all-to-all | bytes 1048576 | tf_op jit(solution)/shard_map/all_to_all | solution.py:200
  39.3 3.7 %collective-permute-start = (bf16[8,4,8,2,512]{4,3,2,1,0:T(2,128)(2,1)S(1)}, bf16[8,4,8,2,512]{4,3,2,1,0:T(2,128)(2,1)S(1)}, u32[]{:S(2)}, u32[]{:S(2)}) collective-permute-start(bf16[8,4,8,2,512]{4,3,2,1,0:T(2,128)(2,1)S(1)} %all_to_all.20.own_ref), channel_id=1, source_target_pairs={{0,1},{1,0},{2,3},{3,2},{4,5},{5,4},{6,7},{7,6},{8,9},{9,8},{10,11... | collective-permute-start | bytes 1572872 | tf_op jit(solution)/shard_map/ppermute | solution.py:201
  43.1 0.0 copy-done
  43.1 0.9 %rows.1.rows_ref = s32[2,2048]{1,0:T(2,128)S(1)} custom-call(bf16[4,4,5,2,512]{4,3,2,1,0:T(2,128)(2,1)} %bitcast.4), custom_call_target="tpu_custom_call" | custom-call | tf_op jit(solution)/shard_map/rows/pallas_call | solution.py:109
  44.0 0.0 copy-start.1
  44.0 0.9 %copy-done.1 = bf16[16,5,2,512]{3,2,1,0:T(2,128)(2,1)S(1)} copy-done((bf16[16,5,2,512]{3,2,1,0:T(2,128)(2,1)S(1)}, bf16[16,5,2,512]{3,2,1,0:T(2,128)(2,1)}, u32[]{:S(2)}) %copy-start.1) | copy-done | bytes 163864
  44.9 1.3 %tables.1.table_ref = f32[2,2048,128]{2,1,0:T(8,128)S(1)} custom-call(bf16[4,4,5,2,512]{4,3,2,1,0:T(2,128)(2,1)S(1)} %bitcast.5), custom_call_target="tpu_custom_call" | custom-call | flops 4194304 | tf_op jit(solution)/shard_map/tables/pallas_call | solution.py:116
  46.2 0.0 collective-permute-done.other_ref
  46.2 12.3 %sums.1 = f32[16,128]{1,0:T(8,128)S(1)} custom-call(s32[2,2048]{1,0:T(2,128)S(1)} %rows.1.rows_ref, f32[2,2048,128]{2,1,0:T(8,128)S(1)} %tables.1.table_ref, bf16[8,4,8,2,512]{4,3,2,1,0:T(2,128)(2,1)S(1)} %all_to_all.20.own_ref, bf16[8,4,8,2,512]{4,3,2,1,0:T(2,128)(2,1)S(1)} %collective-permute-done.other_ref), custom_call_target="tpu_custom_call" | custom-call | flops 4294967296 | tf_op jit(solution)/shard_map/sums/pallas_call | solution.py:174
  58.6 0.1 all_to_all.14
  58.6 9.8 %all_to_all.21 = f32[16,1,512]{2,1,0:T(1,128)S(1)} all-to-all(f32[16,1,512]{2,1,0:T(1,128)S(1)} %all_to_all.14), channel_id=1, replica_groups=mesh['rows'=4,'deep'=8,'side'=4,'core'=2] {'rows','side'}, dimensions={0} | all-to-all | bytes 65536 | tf_op jit(solution)/shard_map/all_to_all | solution.py:206
  68.4 0.6 add_divide_fusion
  (4 shorter events, 0.1 us)
Async XLA Ops:
  16.1 27.0 %copy-start = (bf16[16,5,2,512]{3,2,1,0:T(2,128)(2,1)}, bf16[16,5,2,512]{3,2,1,0:T(2,128)(2,1)S(1)}, u32[]{:S(2)}) copy-start(bf16[16,5,2,512]{3,2,1,0:T(2,128)(2,1)S(1)} %all_to_all.19) | copy-start | bytes 491524
  39.3 6.9 %collective-permute-start = (bf16[8,4,8,2,512]{4,3,2,1,0:T(2,128)(2,1)S(1)}, bf16[8,4,8,2,512]{4,3,2,1,0:T(2,128)(2,1)S(1)}, u32[]{:S(2)}, u32[]{:S(2)}) collective-permute-start(bf16[8,4,8,2,512]{4,3,2,1,0:T(2,128)(2,1)S(1)} %all_to_all.20.own_ref), channel_id=1, source_target_pairs={{0,1},{1,0},{2,3},{3,2},{4,5},{5,4},{6,7},{7,6},{8,9},{9,8},{10,11... | collective-permute-start | bytes 1572872 | tf_op jit(solution)/shard_map/ppermute | solution.py:201
  44.0 0.9 %copy-start.1 = (bf16[16,5,2,512]{3,2,1,0:T(2,128)(2,1)S(1)}, bf16[16,5,2,512]{3,2,1,0:T(2,128)(2,1)}, u32[]{:S(2)}) copy-start(bf16[16,5,2,512]{3,2,1,0:T(2,128)(2,1)} %copy-done) | copy-start | bytes 491524

commit v4 on v3

v4 whole, which is shorter than its diff:
```python
import functools

import jax
import jax.numpy as jnp
import numpy as np
from jax import lax
from jax.experimental import pallas as pl
from jax.experimental.pallas import tpu as pltpu
from jax.sharding import Mesh
from jax.sharding import PartitionSpec as P

NOISE = 1920
PHASES = 4096
LATTICE = 64
LANES = 128
BATCH = 32
EXTRA = 4
ROWS, DEEP, SIDE, CORE = "rows", "deep", "side", "core"
GRID = (DEEP, SIDE, CORE)


def sine_coefficients():
    nodes = 0.03125 * (1.0 - np.cos((np.arange(64) + 0.5) * np.pi / 64))
    root = np.sqrt(nodes)
    value = np.sin(2.0 * np.pi * root) / root
    return tuple(float(c) for c in np.polynomial.polynomial.polyfit(nodes, value, 5))


SINE = sine_coefficients()


def sine_of(u):
    square = u * u
    total = jnp.full_like(u, SINE[-1])
    for c in SINE[-2::-1]:
        total = total * square + c
    return total * u


def cos_sin_of(turns):
    rest = turns - jnp.round(turns)
    cos = sine_of(0.25 - jnp.abs(rest))
    sin = sine_of(jnp.maximum(jnp.minimum(rest, 0.5 - rest), -0.5 - rest))
    return cos, sin


def pack_kernel(positions_ref, columns_ref, out_ref):
    row_groups, deep, tiles = out_ref.shape[0], out_ref.shape[1], positions_ref.shape[0]
    quarter, width = (out_ref.shape[2] - 1) // tiles, columns_ref.shape[0]
    mine = positions_ref[lax.rem(lax.axis_index(DEEP), tiles)]
    mine = mine.astype(jnp.float32).astype(out_ref.dtype)
    nothing = jnp.zeros((2, LANES), out_ref.dtype)
    for r in range(row_groups):
        for c in range(quarter):
            column = r * quarter + c
            for t in range(tiles):
                part = columns_ref[column, :, t * LANES : (t + 1) * LANES] if column < width else nothing
                for d in range(deep):
                    out_ref[r, d, t * quarter + c] = part
        for d in range(deep):
            out_ref[r, d, tiles * quarter] = mine


def packed(positions, columns, row_groups, deep):
    width, tiles = columns.shape[0], positions.shape[0]
    pairs = tiles * -(-width // row_groups) + 1
    return pl.pallas_call(
        pack_kernel,
        out_shape=jax.ShapeDtypeStruct((row_groups, deep, pairs, 2, LANES), columns.dtype),
        in_specs=[pl.BlockSpec(memory_space=pltpu.VMEM)] * 2,
        out_specs=pl.BlockSpec(memory_space=pltpu.VMEM),
        cost_estimate=pl.CostEstimate(flops=2**16, bytes_accessed=0, transcendentals=0),
        name="pack",
    )(positions, columns)


def rows_kernel(own_ref, rows_ref, *, scale):
    row_groups, _, pairs, _, _ = own_ref.shape
    elements = rows_ref.shape[0] // 2
    tiles = elements // (row_groups * LANES)
    for r in range(row_groups):
        for t in range(tiles):
            part = (own_ref[r, t, pairs - 1].astype(jnp.float32) * scale).astype(jnp.int32)
            for k in range(2):
                here = k * elements + (r * tiles + t) * LANES
                rows_ref[here : here + LANES] = part[k]


def turns_kernel(*refs):
    *angles, turns_ref = refs
    side, share = len(angles), angles[0].shape[1]
    each = share // LANES
    for s, ref in enumerate(angles):
        first = lax.rem(lax.axis_index(SIDE) + side - s, side) * each
        part = ref[...].astype(jnp.float32) * (1.0 / PHASES)
        for j in range(each):
            for k in range(2):
                turns_ref[k, pl.ds(first + j, 1), :] = part[k : k + 1, j * LANES : (j + 1) * LANES]


def tables_kernel(turns_ref, table_ref):
    blocks = turns_ref.shape[1]

    def fill(step, carry):
        for k in range(2):
            cos, sin = cos_sin_of(turns_ref[k] * step.astype(jnp.float32))
            first = pl.multiple_of(2 * step * blocks, 2 * blocks)
            table_ref[k, pl.ds(first, blocks), :] = cos
            table_ref[k, pl.ds(first + blocks, blocks), :] = sin
        return carry

    lax.fori_loop(0, LATTICE, fill, 0, unroll=4)


def rows_of(own, elements, blocks):
    return pl.pallas_call(
        functools.partial(rows_kernel, scale=2 * blocks),
        out_shape=pltpu.VMEM((2 * elements,), jnp.int32),
        in_specs=[pl.BlockSpec(memory_space=pltpu.VMEM)],
        out_specs=pl.BlockSpec(memory_space=pltpu.VMEM),
        name="rows",
    )(own)


def turns_of(angles):
    blocks = len(angles) * angles[0].shape[1] // LANES
    return pl.pallas_call(
        turns_kernel,
        out_shape=jax.ShapeDtypeStruct((2, blocks, LANES), jnp.float32),
        in_specs=[pl.BlockSpec(memory_space=pltpu.VMEM)] * len(angles),
        out_specs=pl.BlockSpec(memory_space=pltpu.VMEM),
        cost_estimate=pl.CostEstimate(flops=2**16, bytes_accessed=0, transcendentals=0),
        name="turns",
    )(*angles)


def tables_of(turns):
    return pl.pallas_call(
        tables_kernel,
        out_shape=pltpu.VMEM((2, LATTICE * 2 * turns.shape[1], LANES), jnp.float32),
        in_specs=[pl.BlockSpec(memory_space=pltpu.VMEM)],
        out_specs=pl.BlockSpec(memory_space=pltpu.VMEM),
        cost_estimate=pl.CostEstimate(flops=2**22, bytes_accessed=0, transcendentals=0),
        compiler_params=pltpu.CompilerParams(vmem_limit_bytes=4 * 2**20),
        name="tables",
    )(turns)


def sums_kernel(rows_ref, table_ref, own_ref, other_ref, out_ref, steering):
    row_groups, deep, pairs, _, _ = own_ref.shape
    blocks, elements = out_ref.shape[0], rows_ref.shape[0] // 2
    tiles = elements // (row_groups * LANES)
    quarter = (pairs - 1) // tiles
    pitch = elements + EXTRA

    def batch(step, carry):
        first = pl.multiple_of(step * BATCH, BATCH)
        for e in range(BATCH):
            one = pl.multiple_of(rows_ref[first + e], 2 * blocks)
            two = pl.multiple_of(rows_ref[elements + first + e], 2 * blocks)
            cos_one, sin_one = jnp.split(table_ref[0, pl.ds(one, 2 * blocks), :], 2)
            cos_two, sin_two = jnp.split(table_ref[1, pl.ds(two, 2 * blocks), :], 2)
            here = pl.ds(first + e, blocks, stride=pitch)
            steering[0, here, :] = cos_one * cos_two - sin_one * sin_two
            steering[1, here, :] = sin_one * cos_two + cos_one * sin_two
        return carry

    lax.fori_loop(0, elements // BATCH, batch, 0)

    weights = [
        [
            ref[r, d, t * quarter : (t + 1) * quarter].reshape(2 * quarter, LANES)
            for r in range(row_groups)
            for t in range(tiles)
        ]
        for ref in (own_ref, other_ref)
        for d in range(deep)
    ]
    weights = jnp.concatenate([jnp.concatenate(part, 1) for part in weights], 0)
    is_real = lax.broadcasted_iota(jnp.int32, (8, LANES), 0) % 2 == 0
    for b in range(blocks):
        both = [
            steering[k, b * pitch : b * pitch + elements, :].astype(weights.dtype) for k in range(2)
        ]
        both = jnp.concatenate(both, 1)
        product = jnp.dot(weights, both, preferred_element_type=jnp.float32)
        total = jnp.zeros((8, LANES), jnp.float32)
        for g in range(0, product.shape[0], 8):
            cos, sin = product[g : g + 8, :LANES], product[g : g + 8, LANES:]
            real = cos + pltpu.roll(sin, 7, 0)
            imag = sin - pltpu.roll(cos, 7, 0)
            total = total + (real * real + imag * imag)
        out_ref[b : b + 1, :] = jnp.sum(jnp.where(is_real, total, 0.0), 0, keepdims=True)


def sums_of(table, rows, own, other):
    blocks = table.shape[1] // (2 * LATTICE)
    return pl.pallas_call(
        sums_kernel,
        out_shape=jax.ShapeDtypeStruct((blocks, LANES), jnp.float32),
        in_specs=[pl.BlockSpec(memory_space=pltpu.SMEM)]
        + [pl.BlockSpec(memory_space=pltpu.VMEM)] * 3,
        out_specs=pl.BlockSpec(memory_space=pltpu.VMEM),
        scratch_shapes=[pltpu.VMEM((2, blocks * (rows.size // 2 + EXTRA), LANES), jnp.float32)],
        cost_estimate=pl.CostEstimate(
            flops=8 * own.size * blocks * LANES, bytes_accessed=0, transcendentals=0
        ),
        compiler_params=pltpu.CompilerParams(vmem_limit_bytes=36 * 2**20),
        name="sums",
    )(rows, table, own, other)


def spectrum_of(positions, angles, subspace):
    rows, side, deep = lax.axis_size(ROWS), lax.axis_size(SIDE), lax.axis_size(DEEP)
    tiles = positions.shape[1] // LANES
    coordinates = positions.reshape(2, tiles, LANES).transpose(1, 0, 2)
    pieces = packed(coordinates, subspace.transpose(2, 0, 1), rows, deep)
    own = lax.all_to_all(
        pieces.reshape(rows * deep, *pieces.shape[2:]), (ROWS, DEEP), 0, 0, tiled=True
    )
    turned = [angles]
    for step in range(1, side):
        moves = [(s, (s + step) % side) for s in range(side)]
        turned.append(lax.ppermute(angles, SIDE, moves))
    other = lax.ppermute(own, CORE, [(0, 1), (1, 0)])
    own, other = (part.reshape(pieces.shape) for part in (own, other))

    table = tables_of(turns_of(turned))
    table_rows = rows_of(own, rows * positions.shape[1], table.shape[1] // (2 * LATTICE))
    sums = sums_of(table, table_rows, own, other).reshape(1, side, -1)
    sums = jnp.broadcast_to(sums, (rows, *sums.shape[1:]))
    parts = lax.all_to_all(sums.reshape(rows * side, -1), (ROWS, SIDE), 0, 0, tiled=True)
    return 1.0 / (jnp.sum(parts, 0) / NOISE + 1e-06)


def solution(mesh):
    split = Mesh(mesh.devices.reshape(mesh.shape["rows"], 8, 4, 2), (ROWS, *GRID))
    in_specs = (P(None, ROWS), P(None, GRID), P(None, ROWS, GRID))
    return jax.shard_map(spectrum_of, mesh=split, in_specs=in_specs, out_specs=P(GRID), check_vma=False)
```

time: 69.3 us -> 68.2 us (0.984)
  the two profiles are of different devices: /device:TPU:1 before, /device:TPU:32 now
where the time goes in v4:
time: 68.2 us; the launch traced here: 67.8 us
  blocking collectives  41.3 us (61%)
  Pallas kernels  15.1 us (22%)
  starting transfers between devices  5.83 us (9%)
  waiting for transfers between devices  2.47 us (4%)
  local copies, waits for them, and re-layouts  2.43 us (4%)
    all_to_all x1, blocking collectives, spectrum_of(): lax.all_to_all(pieces.reshape(rows * deep, *pieces.shape[2:]), (ROWS, DEE...  29.1 us
    all_to_all x1, blocking collectives, spectrum_of(): lax.all_to_all(sums.reshape(rows * side, -1), (ROWS, SIDE), 0, 0, tiled=T...  12.2 us
    pallas_call x1, Pallas kernels, sums_of(): pl.pallas_call(sums_kernel, out_shape=jax.ShapeDtypeStruct((blocks, LANES...  9.51 us
    ppermute x3, starting transfers between devices, spectrum_of(): turned.append(lax.ppermute(angles, SIDE, moves))  5.83 us
    ppermute x3, waiting for transfers between devices, spectrum_of(): turned.append(lax.ppermute(angles, SIDE, moves))  2.46 us
    unnamed x12, local copies, waits for them, and re-layouts  2.36 us
    pallas_call x1, Pallas kernels, packed(): pl.pallas_call(pack_kernel, out_shape=jax.ShapeDtypeStruct((row_groups, d...  1.93 us
  transfers between devices with their start and end apart: 4, of which 2 were waited for; matrix products, arithmetic and copies ran while one was open for 0% of the time, Pallas kernels for 5%

profile of v4, /device:TPU:32, one launch (start us, length us, event | category | flops | bytes accessed | tf_op | source)
XLA Modules:
  0.0 67.8 jit_solution(18053795236929947654)
XLA Ops:
  0.0 1.9 %pack.1 = bf16[4,8,33,2,128]{4,3,2,1,0:T(2,128)(2,1)} custom-call(s32[4,2,128]{2,1,0:T(2,128)} %bitcast.12, bf16[30,2,512]{2,1,0:T(2,128)(2,1)} %bitcast.11), custom_call_target="tpu_custom_call" | custom-call | flops 65536 | tf_op jit(solution)/shard_map/pack/pallas_call | solution.py:67
  1.9 29.1 %all_to_all.14 = bf16[32,33,2,128]{3,2,1,0:T(2,128)(2,1)S(1)} all-to-all(bf16[32,33,2,128]{3,2,1,0:T(2,128)(2,1)} %bitcast.10), channel_id=1, replica_groups=mesh['rows'=4,'deep'=8,'side'=4,'core'=2] {'rows','deep'}, dimensions={0} | all-to-all | bytes 1081344 | tf_op jit(solution)/shard_map/all_to_all | solution.py:218
  31.0 0.0 copy-start
  31.0 0.0 collective-permute-start.3
  31.0 1.6 %collective-permute-start = (s32[2,512]{1,0:T(2,128)}, s32[2,512]{1,0:T(2,128)S(1)}, u32[]{:S(2)}, u32[]{:S(2)}) collective-permute-start(s32[2,512]{1,0:T(2,128)} %refs_0_.1), channel_id=1, source_target_pairs={{0,2},{2,4},{4,6},{6,0},{1,3},{3,5},{5,7},{7,1},{8,10},{10,12},{12... | collective-permute-start | bytes 12296 | tf_op jit(solution)/shard_map/ppermute | solution.py:224
  32.6 2.9 %collective-permute-start.1 = (s32[2,512]{1,0:T(2,128)}, s32[2,512]{1,0:T(2,128)S(1)}, u32[]{:S(2)}, u32[]{:S(2)}) collective-permute-start(s32[2,512]{1,0:T(2,128)} %refs_0_.1), channel_id=1, source_target_pairs={{0,4},{2,6},{4,0},{6,2},{1,5},{3,7},{5,1},{7,3},{8,12},{10,14},{12... | collective-permute-start | bytes 12296 | tf_op jit(solution)/shard_map/ppermute | solution.py:224
  35.5 1.3 %collective-permute-start.2 = (s32[2,512]{1,0:T(2,128)}, s32[2,512]{1,0:T(2,128)S(1)}, u32[]{:S(2)}, u32[]{:S(2)}) collective-permute-start(s32[2,512]{1,0:T(2,128)} %refs_0_.1), channel_id=1, source_target_pairs={{0,6},{2,0},{4,2},{6,4},{1,7},{3,1},{5,3},{7,5},{8,14},{10,8},{12,... | collective-permute-start | bytes 12296 | tf_op jit(solution)/shard_map/ppermute | solution.py:224
  36.9 0.0 collective-permute-done.refs_1_
  36.9 0.0 copy-start.3
  36.9 1.1 %collective-permute-done.1.refs_2_ = s32[2,512]{1,0:T(2,128)S(1)} collective-permute-done((s32[2,512]{1,0:T(2,128)}, s32[2,512]{1,0:T(2,128)S(1)}, u32[]{:S(2)}, u32[]{:S(2)}) %collective-permute-start.1) | collective-permute-done | bytes 4128 | tf_op jit(solution)/shard_map/ppermute | solution.py:224
  37.9 0.0 copy-start.4
  37.9 1.4 %collective-permute-done.2.refs_3_ = s32[2,512]{1,0:T(2,128)S(1)} collective-permute-done((s32[2,512]{1,0:T(2,128)}, s32[2,512]{1,0:T(2,128)S(1)}, u32[]{:S(2)}, u32[]{:S(2)}) %collective-permute-start.2) | collective-permute-done | bytes 4128 | tf_op jit(solution)/shard_map/ppermute | solution.py:224
  39.3 0.0 copy-done.3
  39.3 0.0 copy-done.4
  39.3 0.0 copy-start.5
  39.3 0.6 copy-done.5
  39.9 1.3 %turns.1.turns_ref = f32[2,16,128]{2,1,0:T(8,128)} custom-call(s32[2,512]{1,0:T(2,128)} %refs_0_.1, s32[2,512]{1,0:T(2,128)} %copy-done.3, s32[2,512]{1,0:T(2,128)} %copy-done.4, s32[2,512]{1,0:T(2,128)} %copy-done.5), custom_call_target="tpu_custom_call" | custom-call | flops 65536 | tf_op jit(solution)/shard_map/turns/pallas_call | solution.py:127
  41.3 0.0 copy-start.2
  41.3 0.7 %copy-done.2 = f32[2,16,128]{2,1,0:T(8,128)S(1)} copy-done((f32[2,16,128]{2,1,0:T(8,128)S(1)}, f32[2,16,128]{2,1,0:T(8,128)}, u32[]{:S(2)}) %copy-start.2) | copy-done | bytes 16408
  42.0 1.2 %tables.1.table_ref = f32[2,2048,128]{2,1,0:T(8,128)S(1)} custom-call(f32[2,16,128]{2,1,0:T(8,128)S(1)} %copy-done.2), custom_call_target="tpu_custom_call" | custom-call | flops 4194304 | tf_op jit(solution)/shard_map/tables/pallas_call | solution.py:138
  43.2 0.0 copy-done
  43.2 1.1 %rows.1.rows_ref = s32[4096]{0:T(1024)S(1)} custom-call(bf16[4,8,33,2,128]{4,3,2,1,0:T(2,128)(2,1)} %bitcast.7), custom_call_target="tpu_custom_call" | custom-call | tf_op jit(solution)/shard_map/rows/pallas_call | solution.py:116
  44.3 0.0 collective-permute-done.3
  44.3 0.0 copy-start.1
  44.3 1.0 %copy-done.1 = bf16[32,33,2,128]{3,2,1,0:T(2,128)(2,1)S(1)} copy-done((bf16[32,33,2,128]{3,2,1,0:T(2,128)(2,1)S(1)}, bf16[32,33,2,128]{3,2,1,0:T(2,128)(2,1)}, u32[]{:S(2)}) %copy-start.1) | copy-done | bytes 540696
  45.4 9.5 %sums.1 = f32[16,128]{1,0:T(8,128)S(1)} custom-call(s32[4096]{0:T(1024)S(1)} %rows.1.rows_ref, f32[2,2048,128]{2,1,0:T(8,128)S(1)} %tables.1.table_ref, bf16[4,8,33,2,128]{4,3,2,1,0:T(2,128)(2,1)S(1)} %bitcast.8, bf16[4,8,33,2,128]{4,3,2,1,0:T(2,128)(2,1)S(1)} %bitcast.9), custom_call_target="tpu_custom_call" | custom-call | flops 4429185024 | tf_op jit(solution)/shard_map/sums/pallas_call | solution.py:198
  54.9 0.1 all_to_all.10
  55.0 12.2 %all_to_all.15 = f32[16,1,512]{2,1,0:T(1,128)S(1)} all-to-all(f32[16,1,512]{2,1,0:T(1,128)S(1)} %all_to_all.10), channel_id=1, replica_groups=mesh['rows'=4,'deep'=8,'side'=4,'core'=2] {'rows','side'}, dimensions={0} | all-to-all | bytes 65536 | tf_op jit(solution)/shard_map/all_to_all | solution.py:232
  67.2 0.6 add_divide_fusion
  (3 shorter events, 0.1 us)
Async XLA Ops:
  31.0 12.2 %copy-start = (bf16[32,33,2,128]{3,2,1,0:T(2,128)(2,1)}, bf16[32,33,2,128]{3,2,1,0:T(2,128)(2,1)S(1)}, u32[]{:S(2)}) copy-start(bf16[32,33,2,128]{3,2,1,0:T(2,128)(2,1)S(1)} %all_to_all.14) | copy-start | bytes 1622020
  31.0 13.3 %collective-permute-start.3 = (bf16[32,33,2,128]{3,2,1,0:T(2,128)(2,1)S(1)}, bf16[32,33,2,128]{3,2,1,0:T(2,128)(2,1)S(1)}, u32[]{:S(2)}, u32[]{:S(2)}) collective-permute-start(bf16[32,33,2,128]{3,2,1,0:T(2,128)(2,1)S(1)} %all_to_all.14), channel_id=1, source_target_pairs={{0,1},{1,0},{2,3},{3,2},{4,5},{5,4},{6,7},{7,6},{8,9},{9,8},{10,11... | collective-permute-start | bytes 1622024 | tf_op jit(solution)/shard_map/ppermute | solution.py:225
  31.0 5.8 %collective-permute-start = (s32[2,512]{1,0:T(2,128)}, s32[2,512]{1,0:T(2,128)S(1)}, u32[]{:S(2)}, u32[]{:S(2)}) collective-permute-start(s32[2,512]{1,0:T(2,128)} %refs_0_.1), channel_id=1, source_target_pairs={{0,2},{2,4},{4,6},{6,0},{1,3},{3,5},{5,7},{7,1},{8,10},{10,12},{12... | collective-permute-start | bytes 12296 | tf_op jit(solution)/shard_map/ppermute | solution.py:224
  32.6 5.3 %collective-permute-start.1 = (s32[2,512]{1,0:T(2,128)}, s32[2,512]{1,0:T(2,128)S(1)}, u32[]{:S(2)}, u32[]{:S(2)}) collective-permute-start(s32[2,512]{1,0:T(2,128)} %refs_0_.1), channel_id=1, source_target_pairs={{0,4},{2,6},{4,0},{6,2},{1,5},{3,7},{5,1},{7,3},{8,12},{10,14},{12... | collective-permute-start | bytes 12296 | tf_op jit(solution)/shard_map/ppermute | solution.py:224
  35.5 3.8 %collective-permute-start.2 = (s32[2,512]{1,0:T(2,128)}, s32[2,512]{1,0:T(2,128)S(1)}, u32[]{:S(2)}, u32[]{:S(2)}) collective-permute-start(s32[2,512]{1,0:T(2,128)} %refs_0_.1), channel_id=1, source_target_pairs={{0,6},{2,0},{4,2},{6,4},{1,7},{3,1},{5,3},{7,5},{8,14},{10,8},{12,... | collective-permute-start | bytes 12296 | tf_op jit(solution)/shard_map/ppermute | solution.py:224
  36.9 2.5 %copy-start.3 = (s32[2,512]{1,0:T(2,128)}, s32[2,512]{1,0:T(2,128)S(1)}, u32[]{:S(2)}) copy-start(s32[2,512]{1,0:T(2,128)S(1)} %collective-permute-done.refs_1_) | copy-start | bytes 12292
  37.9 1.4 %copy-start.4 = (s32[2,512]{1,0:T(2,128)}, s32[2,512]{1,0:T(2,128)S(1)}, u32[]{:S(2)}) copy-start(s32[2,512]{1,0:T(2,128)S(1)} %collective-permute-done.1.refs_2_) | copy-start | bytes 12292
  39.3 0.6 copy-start.5
  41.3 0.7 %copy-start.2 = (f32[2,16,128]{2,1,0:T(8,128)S(1)}, f32[2,16,128]{2,1,0:T(8,128)}, u32[]{:S(2)}) copy-start(f32[2,16,128]{2,1,0:T(8,128)} %turns.1.turns_ref) | copy-start | bytes 49156
  44.3 1.0 %copy-start.1 = (bf16[32,33,2,128]{3,2,1,0:T(2,128)(2,1)S(1)}, bf16[32,33,2,128]{3,2,1,0:T(2,128)(2,1)}, u32[]{:S(2)}) copy-start(bf16[32,33,2,128]{3,2,1,0:T(2,128)(2,1)} %copy-done) | copy-start | bytes 1622020

commit v5 on v4

v5 whole, which is shorter than its diff:
```python
import jax
import jax.numpy as jnp
import numpy as np
from jax import lax
from jax.experimental import pallas as pl
from jax.experimental.pallas import tpu as pltpu
from jax.sharding import Mesh
from jax.sharding import PartitionSpec as P

NOISE = 1920
PHASES = 4096
LATTICE = 64
LANES = 128
BATCH = 32
PITCH = BATCH + 4
ROWS, FAR, NEAR, SIDE, CORE = "rows", "far", "near", "side", "core"
GRID = (FAR, NEAR, SIDE, CORE)


def sine_coefficients():
    nodes = 0.03125 * (1.0 - np.cos((np.arange(64) + 0.5) * np.pi / 64))
    root = np.sqrt(nodes)
    value = np.sin(2.0 * np.pi * root) / root
    return tuple(float(c) for c in np.polynomial.polynomial.polyfit(nodes, value, 5))


SINE = sine_coefficients()


def sine_of(u):
    square = u * u
    total = jnp.full_like(u, SINE[-1])
    for c in SINE[-2::-1]:
        total = total * square + c
    return total * u


def cos_sin_of(turns):
    rest = turns - jnp.round(turns)
    cos = sine_of(0.25 - jnp.abs(rest))
    sin = sine_of(jnp.maximum(jnp.minimum(rest, 0.5 - rest), -0.5 - rest))
    return cos, sin


def pack_kernel(positions_ref, columns_ref, out_ref):
    row_groups, far, tiles = out_ref.shape[0], out_ref.shape[1], positions_ref.shape[0]
    quarter, width = (out_ref.shape[2] - 1) // tiles, columns_ref.shape[0]
    mine = positions_ref[lax.axis_index(FAR)].astype(jnp.float32).astype(out_ref.dtype)
    nothing = jnp.zeros((2, LANES), out_ref.dtype)
    for r in range(row_groups):
        for c in range(quarter):
            column = r * quarter + c
            for t in range(tiles):
                part = columns_ref[column, :, t * LANES : (t + 1) * LANES] if column < width else nothing
                for d in range(far):
                    out_ref[r, d, t * quarter + c] = part
        for d in range(far):
            out_ref[r, d, tiles * quarter] = mine


def packed(positions, columns, row_groups, far):
    width, tiles = columns.shape[0], positions.shape[0]
    assert tiles == far
    pairs = tiles * -(-width // row_groups) + 1
    return pl.pallas_call(
        pack_kernel,
        out_shape=jax.ShapeDtypeStruct((row_groups, far, pairs, 2, LANES), columns.dtype),
        in_specs=[pl.BlockSpec(memory_space=pltpu.VMEM)] * 2,
        out_specs=pl.BlockSpec(memory_space=pltpu.VMEM),
        cost_estimate=pl.CostEstimate(flops=2**16, bytes_accessed=0, transcendentals=0),
        compiler_params=pltpu.CompilerParams(vmem_limit_bytes=2**20),
        name="pack",
    )(positions, columns)


def tables_kernel(*refs):
    *angles, table_ref, turns = refs
    side, share = len(angles), angles[0].shape[1]
    blocks = turns.shape[1]
    each = share // LANES
    for s, ref in enumerate(angles):
        first = lax.rem(lax.axis_index(SIDE) + side - s, side) * each
        part = ref[...].astype(jnp.float32) * (1.0 / PHASES)
        for j in range(each):
            for k in range(2):
                turns[k, pl.ds(first + j, 1), :] = part[k : k + 1, j * LANES : (j + 1) * LANES]

    def fill(step, carry):
        for k in range(2):
            cos, sin = cos_sin_of(turns[k] * step.astype(jnp.float32))
            first = pl.multiple_of(2 * step * blocks, 2 * blocks)
            table_ref[k, pl.ds(first, blocks), :] = cos
            table_ref[k, pl.ds(first + blocks, blocks), :] = sin
        return carry

    lax.fori_loop(0, LATTICE, fill, 0, unroll=4)


def tables_of(angles):
    blocks = len(angles) * angles[0].shape[1] // LANES
    return pl.pallas_call(
        tables_kernel,
        out_shape=jax.ShapeDtypeStruct((2, LATTICE * 2 * blocks, LANES), jnp.float32),
        in_specs=[pl.BlockSpec(memory_space=pltpu.VMEM)] * len(angles),
        out_specs=pl.BlockSpec(memory_space=pltpu.VMEM),
        scratch_shapes=[pltpu.VMEM((2, blocks, LANES), jnp.float32)],
        cost_estimate=pl.CostEstimate(flops=2**22, bytes_accessed=0, transcendentals=0),
        compiler_params=pltpu.CompilerParams(vmem_limit_bytes=4 * 2**20),
        name="tables",
    )(*angles)


def steering_kernel(own_ref, table_ref, out_ref, stage, listed, rows, arrived):
    row_groups, tiles, pairs, _, _ = own_ref.shape
    blocks, elements = out_ref.shape[1:3]
    for r in range(row_groups):
        for t in range(tiles):
            part = (own_ref[r, t, pairs - 1].astype(jnp.float32) * (2 * blocks)).astype(jnp.int32)
            for k in range(2):
                here = k * elements + (r * tiles + t) * LANES
                listed[here : here + LANES] = part[k]
    copy = pltpu.make_async_copy(listed, rows, arrived)
    copy.start()
    copy.wait()

    def batch(step, carry):
        first = pl.multiple_of(step * BATCH, BATCH)
        for e in range(BATCH):
            one = pl.multiple_of(rows[first + e], 2 * blocks)
            two = pl.multiple_of(rows[elements + first + e], 2 * blocks)
            cos_one, sin_one = jnp.split(table_ref[0, pl.ds(one, 2 * blocks), :], 2)
            cos_two, sin_two = jnp.split(table_ref[1, pl.ds(two, 2 * blocks), :], 2)
            here = pl.ds(e, blocks, stride=PITCH)
            stage[0, here, :] = cos_one * cos_two - sin_one * sin_two
            stage[1, here, :] = sin_one * cos_two + cos_one * sin_two
        for k in range(2):
            for b in range(blocks):
                part = stage[k, b * PITCH : b * PITCH + BATCH, :]
                out_ref[k, b, pl.ds(first, BATCH), :] = part.astype(out_ref.dtype)
        return carry

    lax.fori_loop(0, elements // BATCH, batch, 0)


def steering_of(own, table):
    blocks = table.shape[1] // (2 * LATTICE)
    elements = own.shape[0] * own.shape[1] * LANES
    return pl.pallas_call(
        steering_kernel,
        out_shape=pltpu.VMEM((2, blocks, elements, LANES), own.dtype),
        in_specs=[pl.BlockSpec(memory_space=pltpu.VMEM)] * 2,
        out_specs=pl.BlockSpec(memory_space=pltpu.VMEM),
        scratch_shapes=[
            pltpu.VMEM((2, blocks * PITCH, LANES), jnp.float32),
            pltpu.VMEM((2 * elements,), jnp.int32),
            pltpu.SMEM((2 * elements,), jnp.int32),
            pltpu.SemaphoreType.DMA,
        ],
        cost_estimate=pl.CostEstimate(
            flops=64 * blocks * elements * LANES, bytes_accessed=0, transcendentals=0
        ),
        compiler_params=pltpu.CompilerParams(vmem_limit_bytes=6 * 2**20),
        name="steering",
    )(own, table)


def sums_kernel(*refs):
    *pieces, steering_ref, out_ref = refs
    row_groups, far, pairs, _, _ = pieces[0].shape
    tiles = steering_ref.shape[2] // (row_groups * LANES)
    quarter = (pairs - 1) // tiles
    weights = [
        [
            ref[r, d, t * quarter : (t + 1) * quarter].reshape(2 * quarter, LANES)
            for r in range(row_groups)
            for t in range(tiles)
        ]
        for ref in pieces
        for d in range(far)
    ]
    weights = jnp.concatenate([jnp.concatenate(part, 1) for part in weights], 0)
    is_real = lax.broadcasted_iota(jnp.int32, (8, LANES), 0) % 2 == 0
    for b in range(out_ref.shape[0]):
        both = jnp.concatenate([steering_ref[0, b], steering_ref[1, b]], 1)
        product = jnp.dot(weights, both, preferred_element_type=jnp.float32)
        total = jnp.zeros((8, LANES), jnp.float32)
        for g in range(0, product.shape[0], 8):
            cos, sin = product[g : g + 8, :LANES], product[g : g + 8, LANES:]
            real = cos + pltpu.roll(sin, 7, 0)
            imag = sin - pltpu.roll(cos, 7, 0)
            total = total + (real * real + imag * imag)
        out_ref[b : b + 1, :] = jnp.sum(jnp.where(is_real, total, 0.0), 0, keepdims=True)


def sums_of(pieces, steering):
    blocks = steering.shape[1]
    return pl.pallas_call(
        sums_kernel,
        out_shape=jax.ShapeDtypeStruct((blocks, LANES), jnp.float32),
        in_specs=[pl.BlockSpec(memory_space=pltpu.VMEM)] * (len(pieces) + 1),
        out_specs=pl.BlockSpec(memory_space=pltpu.VMEM),
        cost_estimate=pl.CostEstimate(
            flops=8 * len(pieces) * pieces[0].size * blocks * LANES,
            bytes_accessed=0,
            transcendentals=0,
        ),
        compiler_params=pltpu.CompilerParams(vmem_limit_bytes=6 * 2**20),
        name="sums",
    )(*pieces, steering)


def spectrum_of(positions, angles, subspace):
    rows, side, far = lax.axis_size(ROWS), lax.axis_size(SIDE), lax.axis_size(FAR)
    tiles = positions.shape[1] // LANES
    coordinates = positions.reshape(2, tiles, LANES).transpose(1, 0, 2)
    pieces = packed(coordinates, subspace.transpose(2, 0, 1), rows, far)
    own = lax.all_to_all(
        pieces.reshape(rows * far, *pieces.shape[2:]), (ROWS, FAR), 0, 0, tiled=True
    )
    turned = [angles]
    for step in range(1, side):
        moves = [(s, (s + step) % side) for s in range(side)]
        turned.append(lax.ppermute(angles, SIDE, moves))
    shared = [
        lax.ppermute(own, NEAR, [(0, 1), (1, 0)]),
        lax.ppermute(own, (NEAR, CORE), [(0, 3), (3, 0), (1, 2), (2, 1)]),
        lax.ppermute(own, CORE, [(0, 1), (1, 0)]),
    ]
    own, *shared = (part.reshape(pieces.shape) for part in (own, *shared))

    steering = steering_of(own, tables_of(turned))
    sums = sums_of((own, *shared), steering).reshape(1, side, -1)
    sums = jnp.broadcast_to(sums, (rows, *sums.shape[1:]))
    parts = lax.all_to_all(sums.reshape(rows * side, -1), (ROWS, SIDE), 0, 0, tiled=True)
    return 1.0 / (jnp.sum(parts, 0) / NOISE + 1e-06)


def solution(mesh):
    split = Mesh(mesh.devices.reshape(mesh.shape["rows"], 4, 2, 4, 2), (ROWS, *GRID))
    in_specs = (P(None, ROWS), P(None, GRID), P(None, ROWS, GRID))
    return jax.shard_map(spectrum_of, mesh=split, in_specs=in_specs, out_specs=P(GRID), check_vma=False)
```

time: 68.2 us -> 62.5 us (0.916)
  the two profiles are of different devices: /device:TPU:32 before, /device:TPU:8 now
where the time goes in v5:
time: 62.5 us; the launch traced here: 62.1 us
  blocking collectives  36.6 us (59%)
  Pallas kernels  12.8 us (20%)
  starting transfers between devices  6.32 us (10%)
  waiting for transfers between devices  3.46 us (6%)
  local copies, waits for them, and re-layouts  2.27 us (4%)
  other arithmetic  0.63 us (1%)
    all_to_all x1, blocking collectives, spectrum_of(): lax.all_to_all(pieces.reshape(rows * far, *pieces.shape[2:]), (ROWS, FAR)...  24.3 us
    all_to_all x1, blocking collectives, spectrum_of(): lax.all_to_all(sums.reshape(rows * side, -1), (ROWS, SIDE), 0, 0, tiled=T...  12.3 us
    pallas_call x1, Pallas kernels, steering_of(): pl.pallas_call(steering_kernel, out_shape=pltpu.VMEM((2, blocks, elements...  6.66 us
    pallas_call x1, Pallas kernels, sums_of(): pl.pallas_call(sums_kernel, out_shape=jax.ShapeDtypeStruct((blocks, LANES...  4.67 us
    ppermute x3, starting transfers between devices, spectrum_of(): turned.append(lax.ppermute(angles, SIDE, moves))  4.18 us
    ppermute x3, waiting for transfers between devices, spectrum_of(): turned.append(lax.ppermute(angles, SIDE, moves))  3.46 us
    unnamed x6, local copies, waits for them, and re-layouts  2.2 us
    pallas_call x1, Pallas kernels, tables_of(): pl.pallas_call(tables_kernel, out_shape=jax.ShapeDtypeStruct((2, LATTICE...  1.29 us
  transfers between devices with their start and end apart: 6, of which 3 were waited for; matrix products, arithmetic and copies ran while one was open for 0% of the time, Pallas kernels for 13%

profile of v5, /device:TPU:8, one launch (start us, length us, event | category | flops | bytes accessed | tf_op | source)
XLA Modules:
  0.0 62.1 jit_solution(14783144463567149019)
XLA Ops:
  0.0 0.0 copy-start
  0.0 0.8 %copy-done = bf16[2,512,30]{1,0,2:T(2,128)(2,1)S(1)} copy-done((bf16[2,512,30]{1,0,2:T(2,128)(2,1)S(1)}, bf16[2,512,30]{1,0,2:T(2,128)(2,1)}, u32[]{:S(2)}) %copy-start) | copy-done | bytes 61464
  0.8 0.0 copy-start.1
  0.8 0.7 %copy-done.1 = s32[2,512]{1,0:T(2,128)S(1)} copy-done((s32[2,512]{1,0:T(2,128)S(1)}, s32[2,512]{1,0:T(2,128)}, u32[]{:S(2)}) %copy-start.1) | copy-done | bytes 4120
  1.5 0.1 pack.1
  1.7 24.3 %all_to_all.14 = bf16[16,33,2,128]{3,2,1,0:T(2,128)(2,1)S(1)} all-to-all(bf16[16,33,2,128]{3,2,1,0:T(2,128)(2,1)S(1)} %bitcast.9), channel_id=1, replica_groups=mesh['rows'=4,'far'=4,'near'=2,'side'=4,'core'=2] {'rows','far'}, dimensions={0} | all-to-all | bytes 540672 | tf_op jit(solution)/shard_map/all_to_all | solution.py:217
  25.9 1.1 %collective-permute-start = (bf16[16,33,2,128]{3,2,1,0:T(2,128)(2,1)S(1)}, bf16[16,33,2,128]{3,2,1,0:T(2,128)(2,1)S(1)}, u32[]{:S(2)}, u32[]{:S(2)}) collective-permute-start(bf16[16,33,2,128]{3,2,1,0:T(2,128)(2,1)S(1)} %all_to_all.14), channel_id=1, source_target_pairs={{0,8},{8,0},{1,9},{9,1},{2,10},{10,2},{3,11},{11,3},{4,12},{12,4},... | collective-permute-start | bytes 811016 | tf_op jit(solution)/shard_map/ppermute | solution.py:225
  27.0 0.0 collective-permute-start.1
  27.0 1.1 %collective-permute-start.2 = (bf16[16,33,2,128]{3,2,1,0:T(2,128)(2,1)S(1)}, bf16[16,33,2,128]{3,2,1,0:T(2,128)(2,1)S(1)}, u32[]{:S(2)}, u32[]{:S(2)}) collective-permute-start(bf16[16,33,2,128]{3,2,1,0:T(2,128)(2,1)S(1)} %all_to_all.14), channel_id=1, source_target_pairs={{0,1},{1,0},{2,3},{3,2},{4,5},{5,4},{6,7},{7,6},{8,9},{9,8},{10,11... | collective-permute-start | bytes 811016 | tf_op jit(solution)/shard_map/ppermute | solution.py:227
  28.1 1.6 %collective-permute-start.3 = (s32[2,512]{1,0:T(2,128)}, s32[2,512]{1,0:T(2,128)S(1)}, u32[]{:S(2)}, u32[]{:S(2)}) collective-permute-start(s32[2,512]{1,0:T(2,128)} %refs_0_.1), channel_id=1, source_target_pairs={{0,2},{2,4},{4,6},{6,0},{1,3},{3,5},{5,7},{7,1},{8,10},{10,12},{12... | collective-permute-start | bytes 12296 | tf_op jit(solution)/shard_map/ppermute | solution.py:223
  29.7 0.9 %collective-permute-start.4 = (s32[2,512]{1,0:T(2,128)}, s32[2,512]{1,0:T(2,128)S(1)}, u32[]{:S(2)}, u32[]{:S(2)}) collective-permute-start(s32[2,512]{1,0:T(2,128)} %refs_0_.1), channel_id=1, source_target_pairs={{0,4},{2,6},{4,0},{6,2},{1,5},{3,7},{5,1},{7,3},{8,12},{10,14},{12... | collective-permute-start | bytes 12296 | tf_op jit(solution)/shard_map/ppermute | solution.py:223
  30.6 1.3 %collective-permute-done.3.refs_1_ = s32[2,512]{1,0:T(2,128)S(1)} collective-permute-done((s32[2,512]{1,0:T(2,128)}, s32[2,512]{1,0:T(2,128)S(1)}, u32[]{:S(2)}, u32[]{:S(2)}) %collective-permute-start.3) | collective-permute-done | bytes 4128 | tf_op jit(solution)/shard_map/ppermute | solution.py:223
  31.9 1.7 %collective-permute-start.5 = (s32[2,512]{1,0:T(2,128)}, s32[2,512]{1,0:T(2,128)S(1)}, u32[]{:S(2)}, u32[]{:S(2)}) collective-permute-start(s32[2,512]{1,0:T(2,128)} %refs_0_.1), channel_id=1, source_target_pairs={{0,6},{2,0},{4,2},{6,4},{1,7},{3,1},{5,3},{7,5},{8,14},{10,8},{12,... | collective-permute-start | bytes 12296 | tf_op jit(solution)/shard_map/ppermute | solution.py:223
  33.6 1.4 %collective-permute-done.4.refs_2_ = s32[2,512]{1,0:T(2,128)S(1)} collective-permute-done((s32[2,512]{1,0:T(2,128)}, s32[2,512]{1,0:T(2,128)S(1)}, u32[]{:S(2)}, u32[]{:S(2)}) %collective-permute-start.4) | collective-permute-done | bytes 4128 | tf_op jit(solution)/shard_map/ppermute | solution.py:223
  35.0 0.7 %collective-permute-done.5.refs_3_ = s32[2,512]{1,0:T(2,128)S(1)} collective-permute-done((s32[2,512]{1,0:T(2,128)}, s32[2,512]{1,0:T(2,128)S(1)}, u32[]{:S(2)}, u32[]{:S(2)}) %collective-permute-start.5) | collective-permute-done | bytes 4128 | tf_op jit(solution)/shard_map/ppermute | solution.py:223
  35.7 0.0 copy-start.2
  35.7 0.7 %copy-done.2 = s32[2,512]{1,0:T(2,128)S(1)} copy-done((s32[2,512]{1,0:T(2,128)S(1)}, s32[2,512]{1,0:T(2,128)}, u32[]{:S(2)}) %copy-start.2) | copy-done | bytes 4120
  36.4 1.3 %tables.1.table_ref = f32[2,2048,128]{2,1,0:T(8,128)S(1)} custom-call(s32[2,512]{1,0:T(2,128)S(1)} %copy-done.2, s32[2,512]{1,0:T(2,128)S(1)} %collective-permute-done.3.refs_1_, s32[2,512]{1,0:T(2,128)S(1)} %collective-permute-done.4.refs_2_, s32[2,512]{1,0:T(2,128)S(1)} %collective-permute-done.5.refs_3_), custom_call_target="tpu_custom_call" | custom-call | flops 4194304 | tf_op jit(solution)/shard_map/tables/pallas_call | solution.py:101
  37.7 6.7 %steering.1.refs_4_ = bf16[2,16,2048,128]{3,2,1,0:T(8,128)(2,1)S(1)} custom-call(bf16[4,4,33,2,128]{4,3,2,1,0:T(2,128)(2,1)S(1)} %bitcast.10, f32[2,2048,128]{2,1,0:T(8,128)S(1)} %tables.1.table_ref), custom_call_target="tpu_custom_call" | custom-call | flops 268435456 | tf_op jit(solution)/shard_map/steering/pallas_call | solution.py:148
  44.4 0.0 collective-permute-done
  44.4 0.0 collective-permute-done.1
  44.4 0.0 collective-permute-done.2
  44.4 4.7 %sums.1 = f32[16,128]{1,0:T(8,128)S(1)} custom-call(bf16[4,4,33,2,128]{4,3,2,1,0:T(2,128)(2,1)S(1)} %bitcast.11, bf16[4,4,33,2,128]{4,3,2,1,0:T(2,128)(2,1)S(1)} %bitcast.14, bf16[4,4,33,2,128]{4,3,2,1,0:T(2,128)(2,1)S(1)} %bitcast.15, bf16[4,4,33,2,128]{4,3,2,1,0:T(2,128)(2,1)S(1)} %bitcast.16, bf16[2,16,2048,128]{3,2,1,0:T(8,128)(2,1)S(1)} %steering.1.refs_4_), custom_call_target="tpu_custom_call" | custom-call | flops 8858370048 | tf_op jit(solution)/shard_map/sums/pallas_call | solution.py:197
  49.1 0.1 all_to_all.10
  49.2 12.3 %all_to_all.15 = f32[16,1,512]{2,1,0:T(1,128)S(1)} all-to-all(f32[16,1,512]{2,1,0:T(1,128)S(1)} %all_to_all.10), channel_id=1, replica_groups=mesh['rows'=4,'far'=4,'near'=2,'side'=4,'core'=2] {'rows','side'}, dimensions={0} | all-to-all | bytes 65536 | tf_op jit(solution)/shard_map/all_to_all | solution.py:234
  61.5 0.6 add_divide_fusion
  (3 shorter events, 0.1 us)
Async XLA Ops:
  0.0 0.8 %copy-start = (bf16[2,512,30]{1,0,2:T(2,128)(2,1)S(1)}, bf16[2,512,30]{1,0,2:T(2,128)(2,1)}, u32[]{:S(2)}) copy-start(bf16[2,512,30]{1,0,2:T(2,128)(2,1)} %param.5) | copy-start | bytes 184324
  0.8 0.7 %copy-start.1 = (s32[2,512]{1,0:T(2,128)S(1)}, s32[2,512]{1,0:T(2,128)}, u32[]{:S(2)}) copy-start(s32[2,512]{1,0:T(2,128)} %param.3) | copy-start | bytes 12292
  25.9 18.4 %collective-permute-start = (bf16[16,33,2,128]{3,2,1,0:T(2,128)(2,1)S(1)}, bf16[16,33,2,128]{3,2,1,0:T(2,128)(2,1)S(1)}, u32[]{:S(2)}, u32[]{:S(2)}) collective-permute-start(bf16[16,33,2,128]{3,2,1,0:T(2,128)(2,1)S(1)} %all_to_all.14), channel_id=1, source_target_pairs={{0,8},{8,0},{1,9},{9,1},{2,10},{10,2},{3,11},{11,3},{4,12},{12,4},... | collective-permute-start | bytes 811016 | tf_op jit(solution)/shard_map/ppermute | solution.py:225
  27.0 17.4 %collective-permute-start.1 = (bf16[16,33,2,128]{3,2,1,0:T(2,128)(2,1)S(1)}, bf16[16,33,2,128]{3,2,1,0:T(2,128)(2,1)S(1)}, u32[]{:S(2)}, u32[]{:S(2)}) collective-permute-start(bf16[16,33,2,128]{3,2,1,0:T(2,128)(2,1)S(1)} %all_to_all.14), channel_id=1, source_target_pairs={{0,9},{9,0},{1,8},{8,1},{2,11},{11,2},{3,10},{10,3},{4,13},{13,4},... | collective-permute-start | bytes 811016 | tf_op jit(solution)/shard_map/ppermute | solution.py:226
  27.0 17.4 %collective-permute-start.2 = (bf16[16,33,2,128]{3,2,1,0:T(2,128)(2,1)S(1)}, bf16[16,33,2,128]{3,2,1,0:T(2,128)(2,1)S(1)}, u32[]{:S(2)}, u32[]{:S(2)}) collective-permute-start(bf16[16,33,2,128]{3,2,1,0:T(2,128)(2,1)S(1)} %all_to_all.14), channel_id=1, source_target_pairs={{0,1},{1,0},{2,3},{3,2},{4,5},{5,4},{6,7},{7,6},{8,9},{9,8},{10,11... | collective-permute-start | bytes 811016 | tf_op jit(solution)/shard_map/ppermute | solution.py:227
  28.1 3.8 %collective-permute-start.3 = (s32[2,512]{1,0:T(2,128)}, s32[2,512]{1,0:T(2,128)S(1)}, u32[]{:S(2)}, u32[]{:S(2)}) collective-permute-start(s32[2,512]{1,0:T(2,128)} %refs_0_.1), channel_id=1, source_target_pairs={{0,2},{2,4},{4,6},{6,0},{1,3},{3,5},{5,7},{7,1},{8,10},{10,12},{12... | collective-permute-start | bytes 12296 | tf_op jit(solution)/shard_map/ppermute | solution.py:223
  29.7 5.3 %collective-permute-start.4 = (s32[2,512]{1,0:T(2,128)}, s32[2,512]{1,0:T(2,128)S(1)}, u32[]{:S(2)}, u32[]{:S(2)}) collective-permute-start(s32[2,512]{1,0:T(2,128)} %refs_0_.1), channel_id=1, source_target_pairs={{0,4},{2,6},{4,0},{6,2},{1,5},{3,7},{5,1},{7,3},{8,12},{10,14},{12... | collective-permute-start | bytes 12296 | tf_op jit(solution)/shard_map/ppermute | solution.py:223
  31.9 3.8 %collective-permute-start.5 = (s32[2,512]{1,0:T(2,128)}, s32[2,512]{1,0:T(2,128)S(1)}, u32[]{:S(2)}, u32[]{:S(2)}) collective-permute-start(s32[2,512]{1,0:T(2,128)} %refs_0_.1), channel_id=1, source_target_pairs={{0,6},{2,0},{4,2},{6,4},{1,7},{3,1},{5,3},{7,5},{8,14},{10,8},{12,... | collective-permute-start | bytes 12296 | tf_op jit(solution)/shard_map/ppermute | solution.py:223
  35.7 0.7 %copy-start.2 = (s32[2,512]{1,0:T(2,128)S(1)}, s32[2,512]{1,0:T(2,128)}, u32[]{:S(2)}) copy-start(s32[2,512]{1,0:T(2,128)} %refs_0_.1) | copy-start | bytes 12292
